TPU v7x, 512 devices: a whole 4x8x8 slice. The times are simulated.
512 devices in a mesh: dp: 16 (over y, core), space: 32 (over z, x).
Axes of the slice: x: 4, y: 8, z: 8, core: 2. Of those that a mesh axis runs over, the one named last changes fastest.
Arguments:
- features: bfloat16 [16, 32, 48, 512], P('dp', 'space'), may hold values from -6 to 6
- device_block: int32 [16, 32], P('dp'), may hold values from 0 to 63, as said below
- conv_first: bfloat16 [48, 27, 48], replicated, may hold values from -0.15625 to 0.15625
- conv_second: bfloat16 [48, 27, 48], replicated, may hold values from -0.15625 to 0.15625
- head_weight: bfloat16 [3, 48], replicated, may hold values from -0.875 to 0.875
- targets: int32 [16, 32, 3, 512], P('dp', 'space'), may hold values 0 or 1
Outputs:
- affinity_logits: float32 [16, 32, 3, 512], P('dp', 'space')
- grad_first: float32 [48, 27, 48], replicated
- grad_second: float32 [48, 27, 48], replicated
- grad_head: float32 [3, 48], replicated
Inputs may be any that keep to these rules, and one draw needn't show every extreme that they name: `device_block`: row n lists 32 distinct block ids of crop n, one for each device; id = (4 * bx + by) * 4 + bz. Blocks that no device lists hold no tissue.
All inputs are finite; a program needn't handle non-finite values. No bound on the sum of `targets` on one device may be relied on, other than what follows from the above.
Results may differ from a plain program's by a relative error of at most 0.0041.
Values may be sent and summed in bfloat16 or wider, within the bound.
A program may use at most 64 MiB of HBM per device.

v0:
```python
import jax
import jax.numpy as jnp
from jax import lax
from jax.sharding import PartitionSpec as P

BS = 8


tap_offsets = [
    (tap_index // 9 - 1, tap_index // 3 % 3 - 1, tap_index % 3 - 1) for tap_index in range(27)
]


def cut_along(array, dim, size):
    shape = array.shape
    parts = array.reshape(*shape[:dim], size, shape[dim] // size, *shape[dim + 1 :])
    return jnp.moveaxis(parts, dim, 0)


def sum_at_owner(array, axis, dim):
    size = lax.axis_size(axis)
    parts = lax.all_to_all(cut_along(array, dim, size), axis, 0, 0, tiled=True)
    return jnp.sum(parts, axis=0)


def sent_to_all(array, axis):
    size = lax.axis_size(axis)
    return lax.all_to_all(
        jnp.broadcast_to(array[None], (size, *array.shape)), axis, 0, 0, tiled=True
    )


def of_everyone(array, axis):
    everything = sent_to_all(array, axis)
    return jnp.sum(everything, axis=0)


def joined_along(parts, dim):
    parts = jnp.moveaxis(parts, 0, dim)
    shape = parts.shape
    return parts.reshape(*shape[:dim], shape[dim] * shape[dim + 1], *shape[dim + 2 :])


def gather_directly(array, axis, dim):
    parts = sent_to_all(array, axis)
    return joined_along(parts, dim)


def elu_pair(values):
    negative = jnp.exp(jnp.minimum(values, 0.0))
    return (jnp.where(values > 0, values, negative - 1.0), jnp.where(values > 0, 1.0, negative))


def neighbor_tables(device_block):
    space_count = lax.axis_size("space")
    depth_z = space_count // 8
    self_index = lax.axis_index("space")
    blocks = device_block[0]
    coords = jnp.stack([blocks // (4 * depth_z), blocks // depth_z % 4, blocks % depth_z])
    own_coords = lax.dynamic_index_in_dim(coords, self_index, 1, keepdims=False)
    offsets = jnp.array(tap_offsets, jnp.int32)
    limits = jnp.array([4, 4, depth_z], jnp.int32)
    wanted = own_coords[None, :] + offsets
    inside = jnp.all((wanted >= 0) & (wanted < limits[None, :]), axis=1) & (jnp.arange(27) != 13)
    wanted_id = (wanted[:, 0] * 4 + wanted[:, 1]) * depth_z + wanted[:, 2]
    matches = (blocks[None, :] == wanted_id[:, None]) & inside[:, None]
    devices = jnp.arange(space_count, dtype=jnp.int32)
    owner_row = jnp.sum(jnp.where(matches, devices[None, :], 0), axis=1)
    present = jnp.any(matches, axis=1)
    relative = coords - own_coords[:, None]
    adjacent = jnp.all(jnp.abs(relative) <= 1, axis=0) & (devices != self_index)
    send_tap = jnp.where(
        adjacent, (relative[0] + 1) * 9 + (relative[1] + 1) * 3 + relative[2] + 1, 13
    )
    return (owner_row, present, send_tap)


def region_slice(block_data, offset, depth_cells):
    span_list = []
    for step_value in offset:
        if step_value == 1:
            span_list.append(slice(BS - depth_cells, BS))
        elif step_value == -1:
            span_list.append(slice(0, depth_cells))
        else:
            span_list.append(slice(0, BS))
    return block_data[:, span_list[0], span_list[1], span_list[2]]


def surround(block_data, depth_cells, tables):
    owner_row, present, send_tap = tables
    channels = block_data.shape[0]
    length = depth_cells * BS * BS
    pieces = []
    for tap_index in range(27):
        if tap_index == 13:
            pieces.append(jnp.zeros((channels, length), block_data.dtype))
        else:
            region = region_slice(block_data, tap_offsets[tap_index], depth_cells).reshape(
                channels, -1
            )
            pieces.append(jnp.pad(region, ((0, 0), (0, length - region.shape[1]))))
    outgoing = jnp.stack(pieces)
    sending = outgoing[send_tap]
    by_source = lax.all_to_all(sending, "space", split_axis=0, concat_axis=0, tiled=True)
    incoming = jnp.where(
        present[:, None, None], by_source[owner_row], jnp.zeros((), block_data.dtype)
    )
    rows_x = []
    for step_x in range(3):
        rows_y = []
        for step_y in range(3):
            rows_z = []
            for step_z in range(3):
                tap_index = step_x * 9 + step_y * 3 + step_z
                if tap_index == 13:
                    rows_z.append(block_data)
                else:
                    extent_list = [
                        BS if step_value == 1 else depth_cells
                        for step_value in (step_x, step_y, step_z)
                    ]
                    count_cells = extent_list[0] * extent_list[1] * extent_list[2]
                    rows_z.append(
                        incoming[tap_index][:, :count_cells].reshape(
                            channels, extent_list[0], extent_list[1], extent_list[2]
                        )
                    )
            rows_y.append(jnp.concatenate(rows_z, axis=3))
        rows_x.append(jnp.concatenate(rows_y, axis=2))
    return jnp.concatenate(rows_x, axis=1)


def conv_padded(padded, kernel, dilation):
    result = lax.conv_general_dilated(
        padded[None],
        kernel,
        (1, 1, 1),
        "VALID",
        rhs_dilation=(dilation, dilation, dilation),
        dimension_numbers=("NCDHW", "OIDHW", "NCDHW"),
        preferred_element_type=jnp.float32,
    )
    return result[0].reshape(kernel.shape[0], BS * BS * BS)


def kernel_grad(padded, grad_rows, dilation):
    channels = padded.shape[0]
    outputs = grad_rows.shape[0]
    grad_block = grad_rows.reshape(outputs, 1, BS, BS, BS)
    result = lax.conv_general_dilated(
        padded[None],
        grad_block,
        (dilation, dilation, dilation),
        "VALID",
        dimension_numbers=("CNDHW", "OIDHW", "NCDHW"),
        preferred_element_type=jnp.float32,
    )
    return result.reshape(channels, outputs, 27).transpose(1, 2, 0)


def on_device(features, device_block, conv_first, conv_second, head_weight, targets):
    channels = features.shape[2]
    tables = neighbor_tables(device_block)
    kernel_first = conv_first.reshape(channels, 3, 3, 3, channels).transpose(0, 4, 1, 2, 3)
    kernel_second = conv_second.reshape(channels, 3, 3, 3, channels).transpose(0, 4, 1, 2, 3)
    block_in = features[0, 0].reshape(channels, BS, BS, BS)
    padded_in = surround(block_in, 1, tables)
    pre_first = conv_padded(padded_in, kernel_first, 1)
    act_first, slope_first = elu_pair(pre_first)
    hid_first = act_first.astype(jnp.bfloat16)
    padded_first = surround(hid_first.reshape(channels, BS, BS, BS), 2, tables)
    pre_second = conv_padded(padded_first, kernel_second, 2)
    act_second, slope_second = elu_pair(pre_second)
    hid_second = act_second.astype(jnp.bfloat16)
    logits = jnp.dot(head_weight, hid_second, preferred_element_type=jnp.float32)
    scale = (lax.axis_size("dp") * lax.axis_size("space") * 3 * BS * BS * BS) ** (-0.5)
    grad_logit = ((jax.nn.sigmoid(logits) - targets[0, 0].astype(jnp.float32)) * scale).astype(
        jnp.bfloat16
    )
    grad_head = lax.dot_general(
        grad_logit, hid_second, (((1,), (1,)), ((), ())), preferred_element_type=jnp.float32
    )
    back_second = lax.dot_general(
        head_weight, grad_logit, (((0,), (0,)), ((), ())), preferred_element_type=jnp.float32
    )
    grad_pre_second = (back_second * slope_second).astype(jnp.bfloat16)
    grad_second = kernel_grad(padded_first, grad_pre_second, 2)
    padded_grad = surround(grad_pre_second.reshape(channels, BS, BS, BS), 2, tables)
    kernel_back = jnp.transpose(kernel_second[:, :, ::-1, ::-1, ::-1], (1, 0, 2, 3, 4))
    back_first = conv_padded(padded_grad, kernel_back, 2)
    grad_pre_first = (back_first * slope_first).astype(jnp.bfloat16)
    grad_first = kernel_grad(padded_in, grad_pre_first, 1)
    flat_grads = jnp.concatenate(
        [grad_first.reshape(-1), grad_second.reshape(-1), grad_head.reshape(-1)]
    )
    space_count = lax.axis_size("space")
    full_len = flat_grads.shape[0]
    padded_len = -(-full_len // space_count) * space_count
    flat_grads = jnp.pad(flat_grads, (0, padded_len - full_len))
    grad_share = sum_at_owner(flat_grads, "space", 0)
    grad_share = of_everyone(grad_share, "dp")
    all_grads = gather_directly(grad_share, "space", 0)
    kernel_len = 27 * channels * channels
    grad_first = all_grads[:kernel_len].reshape(channels, 27, channels)
    grad_second = all_grads[kernel_len : 2 * kernel_len].reshape(channels, 27, channels)
    grad_head = all_grads[2 * kernel_len : 2 * kernel_len + 3 * channels].reshape(3, channels)
    return (logits[None, None], grad_first, grad_second, grad_head)


def solution(mesh):
    in_specs = (
        P("dp", "space", None, None),
        P("dp", None),
        P(),
        P(),
        P(),
        P("dp", "space", None, None),
    )
    out_specs = (P("dp", "space", None, None), P(), P(), P())
    return jax.shard_map(
        on_device, mesh=mesh, in_specs=in_specs, out_specs=out_specs, check_vma=False
    )
```

profile of v0, /device:TPU:1, one launch (start us, length us, event | category | flops | bytes accessed | tf_op | source)
XLA Modules:
  0.0 177.0 jit_solution(10815971793187551046)
XLA Ops:
  0.6 1.0 copy.863
  1.8 0.7 and_select_fusion.3
  2.4 0.2 dynamic-slice_reduce_fusion
  3.2 0.6 gather_fusion
  3.9 0.3 copy.864
  4.2 0.9 reshape.806
  5.1 13.7 %all-to-all-start = ((bf16[32,2,1536]{2,1,0:T(2,128)(2,1)}), bf16[32,2,1536]{2,1,0:T(2,128)(2,1)S(1)}, u32[]{:S(2)}, u32[]{:S(2)}) async-start(bf16[32,2,1536]{2,1,0:T(2,128)(2,1)} %reshape.806), calls=%async_computation | async-start | bytes 393216 | tf_op jit(solution)/shard_map/all_to_all | solution.py:105
  19.0 0.2 select_reduce_fusion
  19.2 0.2 fusion.21
  19.4 9.4 %all-to-all-done = bf16[32,2,1536]{2,1,0:T(2,128)(2,1)S(1)} async-done(((bf16[32,2,1536]{2,1,0:T(2,128)(2,1)}), bf16[32,2,1536]{2,1,0:T(2,128)(2,1)S(1)}, u32[]{:S(2)}, u32[]{:S(2)}) %all-to-all-start) | async-done | bytes 196640 | tf_op jit(solution)/shard_map/all_to_all | solution.py:105
  28.8 0.3 reshape.807
  29.1 0.6 gather_fusion.1
  32.6 0.3 maximum_bitcast_fusion.2
  32.9 3.1 %fusion.12 = f32[1,48,8,8,8]{1,0,4,3,2:T(1,128)S(1)} fusion(bf16[48,3,3,3,48]{4,0,3,2,1:T(8,128)(2,1)S(1)} %bitcast.747, bf16[1,48,10,10,10]{1,4,3,2,0:T(8,128)(2,1)S(1)} %maximum_bitcast_fusion.2), kind=kOutput, calls=%fused_computation.30 | convolution fusion | flops 63700992 | bytes 318720 | tf_op jit(solution)/shard_map/conv_general_dilated | solution.py:135
  39.2 0.6 gather_fusion.2
  39.8 17.2 %all_to_all.36 = bf16[32,48,128]{2,1,0:T(8,128)(2,1)S(1)} all-to-all(bf16[32,48,128]{2,1,0:T(8,128)(2,1)S(1)} %gather_fusion.2), channel_id=1, replica_groups=mesh['dp'=16,'space'=32] {'space'}, dimensions={0} | all-to-all | bytes 786432 | tf_op jit(solution)/shard_map/all_to_all | solution.py:105
  57.0 0.6 gather_fusion.3
  59.5 0.1 copy.918
  60.3 3.4 %maximum_bitcast_fusion = bf16[1,48,12,12,12]{1,4,3,2,0:T(8,128)(2,1)S(1)} fusion(bf16[48,2,2,2]{0,3,2,1:T(2,128)(2,1)S(1)} %bitcast.707, bf16[48,2,2,8]{0,3,2,1:T(8,128)(2,1)S(1)} %bitcast.664, bf16[48,2,2,2]{0,3,2,1:T(2,128)(2,1)S(1)} %bitcast.713, bf16[48,2,8,2]{0,3,2,1:T(2,128)(2,1)S(1)} %bitcast.666, bf16[48,2,8,8]{0,3,2,1:T(8,128)(2,1)S(1)} %bitcast.588, ...), kind=kLoop, calls=%fused_computation.20 | loop fusion | flops 4478976 | bytes 331776 | tf_op jit(solution)/shard_map/broadcast_in_dim | solution.py:136
  63.7 3.4 %fusion.9 = f32[1,48,8,8,8]{1,0,4,3,2:T(1,128)S(1)} fusion(bf16[48,3,3,3,48]{4,0,3,2,1:T(8,128)(2,1)S(1)} %bitcast.559, bf16[1,48,12,12,12]{1,4,3,2,0:T(8,128)(2,1)S(1)} %maximum_bitcast_fusion), kind=kOutput, calls=%fused_computation.18 | convolution fusion | flops 63700992 | bytes 388608 | tf_op jit(solution)/shard_map/conv_general_dilated | solution.py:135
  67.4 0.2 fusion.3
  70.8 1.3 gather_fusion.4
  72.2 6.0 %all-to-all-start.2 = ((bf16[32,48,128]{2,1,0:T(8,128)(2,1)}), bf16[32,48,128]{2,1,0:T(8,128)(2,1)S(1)}, u32[]{:S(2)}, u32[]{:S(2)}) async-start(bf16[32,48,128]{2,1,0:T(8,128)(2,1)} %gather_fusion.4), calls=%async_computation.2 | async-start | bytes 786432 | tf_op jit(solution)/shard_map/all_to_all | solution.py:105
  78.2 3.6 %fusion.7 = f32[48,48,3,3,3]{1,0,4,3,2:T(8,128)S(1)} fusion(bf16[1,48,12,12,12]{1,4,3,2,0:T(8,128)(2,1)S(1)} %maximum_bitcast_fusion, bf16[48,1,8,8,8]{0,4,3,2,1:T(8,128)(2,1)S(1)} %bitcast.570), kind=kOutput, calls=%fused_computation.16 | convolution fusion | flops 63700992 | bytes 463872 | tf_op jit(solution)/shard_map/conv_general_dilated | solution.py:151
  82.0 0.7 copy.1005
  82.7 0.4 reshape.740
  83.1 7.8 %all-to-all-done.2 = bf16[32,48,128]{2,1,0:T(8,128)(2,1)S(1)} async-done(((bf16[32,48,128]{2,1,0:T(8,128)(2,1)}), bf16[32,48,128]{2,1,0:T(8,128)(2,1)S(1)}, u32[]{:S(2)}, u32[]{:S(2)}) %all-to-all-start.2) | async-done | bytes 393248 | tf_op jit(solution)/shard_map/all_to_all | solution.py:105
  90.8 0.6 gather_fusion.5
  94.1 3.6 %maximum_bitcast_fusion.1 = bf16[1,48,12,12,12]{1,4,3,2,0:T(8,128)(2,1)S(1)} fusion(bf16[48,2,2,2]{0,3,2,1:T(2,128)(2,1)S(1)} %bitcast.708, bf16[48,2,2,8]{0,3,2,1:T(8,128)(2,1)S(1)} %bitcast.665, bf16[48,2,2,2]{0,3,2,1:T(2,128)(2,1)S(1)} %bitcast.714, bf16[48,2,8,2]{0,3,2,1:T(2,128)(2,1)S(1)} %bitcast.667, bf16[48,2,8,8]{0,3,2,1:T(8,128)(2,1)S(1)} %bitcast.589, ...), kind=kLoop, calls=%fused_computation.21 | loop fusion | flops 4478976 | bytes 331776 | tf_op jit(solution)/shard_map/broadcast_in_dim | solution.py:136
  97.8 6.8 %fusion.4 = f32[48,48,3,3,3]{1,0,4,3,2:T(8,128)S(1)} fusion(bf16[48,3,3,3,48]{4,0,3,2,1:T(8,128)(2,1)S(1)} %bitcast.560, bf16[1,48,12,12,12]{1,4,3,2,0:T(8,128)(2,1)S(1)} %maximum_bitcast_fusion.1, bf16[1,48,10,10,10]{1,4,3,2,0:T(8,128)(2,1)S(1)} %maximum_bitcast_fusion.2, f32[1,48,8,8,8]{1,0,4,3,2:T(1,128)S(1)} %fusion.12), kind=kOutput, calls=%fused_computation.13 | convolution fusion | flops 127524864 | bytes 733440 | tf_op jit(solution)/shard_map/conv_general_dilated | solution.py:151
  104.6 0.7 copy.1001
  105.3 0.4 reshape.737
  105.8 0.7 all_to_all.26
  106.5 20.2 %all_to_all.37 = f32[32,1,3893]{2,1,0:T(1,128)S(1)} all-to-all(f32[32,1,3893]{2,1,0:T(1,128)S(1)} %all_to_all.26), channel_id=1, replica_groups=mesh['dp'=16,'space'=32] {'space'}, dimensions={0} | all-to-all | bytes 996608 | tf_op jit(solution)/shard_map/all_to_all | solution.py:22
  126.6 0.3 reduce_sum.31
  127.1 22.0 %all_to_all.38 = f32[16,1,3893]{2,1,0:T(1,128)S(1)} all-to-all(f32[16,1,3893]{2,1,0:T(1,128)S(1)} %broadcast_in_dim.99), channel_id=1, replica_groups=mesh['dp'=16,'space'=32] {'dp'}, dimensions={0} | all-to-all | bytes 498304 | tf_op jit(solution)/shard_map/all_to_all | solution.py:28
  149.1 0.2 reduce_sum.32
  149.3 1.0 broadcast_in_dim.100
  150.3 4.5 %all-to-all-start.5 = ((f32[32,1,3893]{2,1,0:T(1,128)}), f32[32,1,3893]{2,1,0:T(1,128)S(1)}, u32[]{:S(2)}, u32[]{:S(2)}) async-start(f32[32,1,3893]{2,1,0:T(1,128)} %broadcast_in_dim.100), calls=%async_computation.5 | async-start | bytes 1015808 | tf_op jit(solution)/shard_map/all_to_all | solution.py:28
  154.9 0.6 copy.1008
  155.5 16.2 %all-to-all-done.5 = f32[32,1,3893]{2,1,0:T(1,128)S(1)} async-done(((f32[32,1,3893]{2,1,0:T(1,128)}), f32[32,1,3893]{2,1,0:T(1,128)S(1)}, u32[]{:S(2)}, u32[]{:S(2)}) %all-to-all-start.5) | async-done | bytes 498336 | tf_op jit(solution)/shard_map/all_to_all | solution.py:28
  171.6 1.2 reduce.11
  172.8 0.2 reshape.742
  173.1 0.7 reshape.745
  173.8 0.4 reshape.744
  174.2 1.2 copy.1010
  175.4 0.4 reshape.743
  175.8 1.2 copy.1009
  (289 shorter events, 15.4 us)
Async XLA Ops:
  0.6 63.0 %copy-start = (bf16[48,27,48]{2,0,1:T(8,128)(2,1)S(1)}, bf16[48,27,48]{2,0,1:T(8,128)(2,1)}, u32[]{:S(2)}) copy-start(bf16[48,27,48]{2,0,1:T(8,128)(2,1)} %param.11) | copy-start | bytes 373252
  3.9 14.9 %copy-start.1 = (s32[27,3]{0,1:T(4,128)S(1)}, s32[27,3]{0,1:T(4,128)}, u32[]{:S(2)}) copy-start(s32[27,3]{0,1:T(4,128)} %constant.94.clone) | copy-start | bytes 976
  3.9 15.1 %copy-start.2 = (s32[1,32]{1,0:T(1,128)S(1)}, s32[1,32]{1,0:T(1,128)}, u32[]{:S(2)}) copy-start(s32[1,32]{1,0:T(1,128)} %param.9) | copy-start | bytes 388
  5.1 23.7 %all-to-all-start = ((bf16[32,2,1536]{2,1,0:T(2,128)(2,1)}), bf16[32,2,1536]{2,1,0:T(2,128)(2,1)S(1)}, u32[]{:S(2)}, u32[]{:S(2)}) async-start(bf16[32,2,1536]{2,1,0:T(2,128)(2,1)} %reshape.806), calls=%async_computation | async-start | bytes 393216 | tf_op jit(solution)/shard_map/all_to_all | solution.py:105
  30.3 2.6 %copy-start.4 = (bf16[48,27,48]{2,0,1:T(8,128)(2,1)S(1)}, bf16[48,27,48]{2,0,1:T(8,128)(2,1)}, u32[]{:S(2)}) copy-start(bf16[48,27,48]{2,0,1:T(8,128)(2,1)} %param.10) | copy-start | bytes 373252
  63.7 3.5 %copy-start.3 = (bf16[3,48]{1,0:T(4,128)(2,1)S(1)}, bf16[3,48]{1,0:T(4,128)(2,1)}, u32[]{:S(2)}) copy-start(bf16[3,48]{1,0:T(4,128)(2,1)} %param.12) | copy-start | bytes 868
  63.7 3.7 %copy-start.5 = (s32[1,1,3,512]{3,1,2,0:T(1,128)S(1)}, s32[1,1,3,512]{3,1,2,0:T(1,128)}, u32[]{:S(2)}) copy-start(s32[1,1,3,512]{3,1,2,0:T(1,128)} %param.13) | copy-start | bytes 18436
  72.2 18.7 %all-to-all-start.2 = ((bf16[32,48,128]{2,1,0:T(8,128)(2,1)}), bf16[32,48,128]{2,1,0:T(8,128)(2,1)S(1)}, u32[]{:S(2)}, u32[]{:S(2)}) async-start(bf16[32,48,128]{2,1,0:T(8,128)(2,1)} %gather_fusion.4), calls=%async_computation.2 | async-start | bytes 786432 | tf_op jit(solution)/shard_map/all_to_all | solution.py:105
  150.3 21.3 %all-to-all-start.5 = ((f32[32,1,3893]{2,1,0:T(1,128)}), f32[32,1,3893]{2,1,0:T(1,128)S(1)}, u32[]{:S(2)}, u32[]{:S(2)}) async-start(f32[32,1,3893]{2,1,0:T(1,128)} %broadcast_in_dim.100), calls=%async_computation.5 | async-start | bytes 1015808 | tf_op jit(solution)/shard_map/all_to_all | solution.py:28
where the time goes:
time: 178 us; the launch traced here: 177 us
  blocking collectives  59.4 us (33%)
  waiting for transfers between devices  33.3 us (19%)
  local copies, waits for them, and re-layouts  30.1 us (17%)
  starting transfers between devices  24.2 us (14%)
  matrix products  17.3 us (10%)
  other arithmetic  10.8 us (6%)
  between operations  1.79 us (1%)
    all_to_all x1, blocking collectives, sent_to_all(): lax.all_to_all(jnp.broadcast_to(array[None], (size, *array.shape)), axis,...  22 us
    all_to_all x1, blocking collectives, sum_at_owner(): parts = lax.all_to_all(cut_along(array, dim, size), axis, 0, 0, tiled=True)  20.2 us
    all_to_all x2, starting transfers between devices, surround(): lax.all_to_all(sending, 'space', split_axis=0, concat_axis=0, tiled=True)  19.7 us
    all_to_all x1, blocking collectives, surround(): lax.all_to_all(sending, 'space', split_axis=0, concat_axis=0, tiled=True)  17.2 us
    all_to_all x2, waiting for transfers between devices, surround(): lax.all_to_all(sending, 'space', split_axis=0, concat_axis=0, tiled=True)  17.2 us
    all_to_all x1, waiting for transfers between devices, sent_to_all(): lax.all_to_all(jnp.broadcast_to(array[None], (size, *array.shape)), axis,...  16.2 us
    conv_general_dilated x2, matrix products, kernel_grad(): lax.conv_general_dilated(padded[None], grad_block, (dilation, dilation, d...  10.4 us
    broadcast_in_dim x3, other arithmetic, conv_padded(): padded[None]  7.31 us
  transfers between devices with their start and end apart: 3, of which 3 were waited for; matrix products, arithmetic and copies ran while one was open for 3% of the time, Pallas kernels for 0%

commit v1 on v0

--- a/solution.py
+++ b/solution.py
@@ -1,6 +1,8 @@
 import jax
 import jax.numpy as jnp
 from jax import lax
+from jax.experimental import pallas as pl
+from jax.experimental.pallas import tpu as pltpu
 from jax.sharding import PartitionSpec as P
 
 BS = 8
@@ -11,39 +13,116 @@
 ]
 
 
-def cut_along(array, dim, size):
-    shape = array.shape
-    parts = array.reshape(*shape[:dim], size, shape[dim] // size, *shape[dim + 1 :])
-    return jnp.moveaxis(parts, dim, 0)
-
-
-def sum_at_owner(array, axis, dim):
-    size = lax.axis_size(axis)
-    parts = lax.all_to_all(cut_along(array, dim, size), axis, 0, 0, tiled=True)
-    return jnp.sum(parts, axis=0)
-
-
-def sent_to_all(array, axis):
-    size = lax.axis_size(axis)
-    return lax.all_to_all(
-        jnp.broadcast_to(array[None], (size, *array.shape)), axis, 0, 0, tiled=True
-    )
-
-
-def of_everyone(array, axis):
-    everything = sent_to_all(array, axis)
-    return jnp.sum(everything, axis=0)
-
-
-def joined_along(parts, dim):
-    parts = jnp.moveaxis(parts, 0, dim)
-    shape = parts.shape
-    return parts.reshape(*shape[:dim], shape[dim] * shape[dim + 1], *shape[dim + 2 :])
-
-
-def gather_directly(array, axis, dim):
-    parts = sent_to_all(array, axis)
-    return joined_along(parts, dim)
+MESH = pl.DeviceIdType.MESH
+
+
+def grad_sum_kernel(g_ref, out_ref, send_buf, rs_buf, dp_buf, ag_buf, send_sem, rs_sem, dp_send, dp_sem, ag_send, ag_sem):
+    dp, sp = lax.axis_index("dp"), lax.axis_index("space")
+    n_dp, n_sp = dp_buf.shape[0], rs_buf.shape[0]
+    rows = rs_buf.shape[1]
+
+    barrier = pltpu.get_barrier_semaphore()
+
+    @pl.loop(1, n_sp)
+    def _(r):
+        pl.semaphore_signal(barrier, inc=1, device_id=(dp, lax.rem(sp + r, n_sp)), device_id_type=MESH)
+
+    @pl.loop(1, n_dp)
+    def _(r):
+        pl.semaphore_signal(barrier, inc=1, device_id=(lax.rem(dp + r, n_dp), sp), device_id_type=MESH)
+
+    send_buf[...] = g_ref[...].reshape(send_buf.shape).astype(jnp.bfloat16)
+    pl.semaphore_wait(barrier, n_sp + n_dp - 2)
+
+    def rs_copy(r):
+        peer = lax.rem(sp + r, n_sp)
+        return pltpu.make_async_remote_copy(
+            src_ref=send_buf.at[peer], dst_ref=rs_buf.at[r], send_sem=send_sem.at[r], recv_sem=rs_sem.at[r],
+            device_id=(dp, peer), device_id_type=MESH)
+
+    def dp_copy(r):
+        peer = lax.rem(dp + r, n_dp)
+        return pltpu.make_async_remote_copy(
+            src_ref=dp_buf.at[0], dst_ref=dp_buf.at[r], send_sem=dp_send.at[r], recv_sem=dp_sem.at[r],
+            device_id=(peer, sp), device_id_type=MESH)
+
+    def ag_copy(r):
+        peer = lax.rem(sp + r, n_sp)
+        return pltpu.make_async_remote_copy(
+            src_ref=ag_buf.at[0], dst_ref=ag_buf.at[r], send_sem=ag_send.at[r], recv_sem=ag_sem.at[r],
+            device_id=(dp, peer), device_id_type=MESH)
+
+    @pl.loop(1, n_sp)
+    def _(r):
+        rs_copy(r).start()
+
+    def add_rs(r, total):
+        rs_copy(r).wait_recv()
+        return total + rs_buf[r].astype(jnp.float32)
+
+    own = g_ref[pl.ds(pl.multiple_of(sp * rows, rows), rows), :]
+    total = lax.fori_loop(1, n_sp, add_rs, own)
+    dp_buf[0] = total.astype(jnp.bfloat16)
+
+    @pl.loop(1, n_dp)
+    def _(r):
+        dp_copy(r).start()
+
+    @pl.loop(1, n_dp)
+    def _(r):
+        dp_copy(r).wait_recv()
+
+    def add_dp(d, total):
+        return total + dp_buf[lax.rem(dp - d + n_dp, n_dp)].astype(jnp.float32)
+
+    total = lax.fori_loop(0, n_dp, add_dp, jnp.zeros((rows, 128), jnp.float32))
+    ag_buf[0] = total.astype(jnp.bfloat16)
+
+    @pl.loop(1, n_sp)
+    def _(r):
+        ag_copy(r).start()
+
+    @pl.loop(1, n_sp)
+    def _(r):
+        rs_copy(r).wait_send()
+
+    @pl.loop(1, n_dp)
+    def _(r):
+        dp_copy(r).wait_send()
+
+    out_ref[pl.ds(pl.multiple_of(sp * rows, rows), rows), :] = ag_buf[0].astype(jnp.float32)
+
+    @pl.loop(1, n_sp)
+    def _(r):
+        ag_copy(r).wait_recv()
+        source = lax.rem(sp - r + n_sp, n_sp)
+        out_ref[pl.ds(pl.multiple_of(source * rows, rows), rows), :] = ag_buf[r].astype(jnp.float32)
+
+    @pl.loop(1, n_sp)
+    def _(r):
+        ag_copy(r).wait_send()
+
+
+def grad_sum(flat):
+    n_dp, n_sp = lax.axis_size("dp"), lax.axis_size("space")
+    total_rows = flat.shape[0]
+    rows = total_rows // n_sp
+    vmem = pl.BlockSpec(memory_space=pltpu.VMEM)
+    dma = pltpu.SemaphoreType.DMA
+    return pl.pallas_call(
+        grad_sum_kernel,
+        out_shape=jax.ShapeDtypeStruct((total_rows, 128), jnp.float32),
+        in_specs=[vmem],
+        out_specs=vmem,
+        scratch_shapes=[
+            pltpu.VMEM((n_sp, rows, 128), jnp.bfloat16),
+            pltpu.VMEM((n_sp, rows, 128), jnp.bfloat16),
+            pltpu.VMEM((n_dp, rows, 128), jnp.bfloat16),
+            pltpu.VMEM((n_sp, rows, 128), jnp.bfloat16),
+            dma((n_sp,)), dma((n_sp,)), dma((n_dp,)), dma((n_dp,)), dma((n_sp,)), dma((n_sp,)),
+        ],
+        compiler_params=pltpu.CompilerParams(collective_id=0, has_side_effects=True),
+    )(flat)
 
 
 def elu_pair(values):
@@ -194,13 +273,11 @@
     flat_grads = jnp.concatenate(
         [grad_first.reshape(-1), grad_second.reshape(-1), grad_head.reshape(-1)]
     )
-    space_count = lax.axis_size("space")
     full_len = flat_grads.shape[0]
-    padded_len = -(-full_len // space_count) * space_count
+    chunk = 16 * 128 * lax.axis_size("space")
+    padded_len = -(-full_len // chunk) * chunk
     flat_grads = jnp.pad(flat_grads, (0, padded_len - full_len))
-    grad_share = sum_at_owner(flat_grads, "space", 0)
-    grad_share = of_everyone(grad_share, "dp")
-    all_grads = gather_directly(grad_share, "space", 0)
+    all_grads = grad_sum(flat_grads.reshape(-1, 128)).reshape(-1)
     kernel_len = 27 * channels * channels
     grad_first = all_grads[:kernel_len].reshape(channels, 27, channels)
     grad_second = all_grads[kernel_len : 2 * kernel_len].reshape(channels, 27, channels)

time: 178 us -> 149 us (0.84); the launches traced: 177 us -> 146 us
  blocking collectives: 59.4 us -> 17.2 us
  Pallas kernels: 0 us -> 33.9 us
  waiting for transfers between devices: 33.3 us -> 16.5 us
  starting transfers between devices: 24.2 us -> 19.7 us
    all_to_all x2 -> x0, blocking collectives: 42.2 us -> none  [the longest x1 22 us: sent_to_all(): lax.all_to_all(jnp.broadcast_to(array[None], (size, *array.shape)), axis,...]
    pallas_call x0 -> x1, Pallas kernels: none -> 33.9 us  [grad_sum(): pl.pallas_call(grad_sum_kernel, out_shape=jax.ShapeDtypeStruct((total_row...]
    all_to_all x1 -> x0, waiting for transfers between devices: 16.2 us -> none  [sent_to_all(): lax.all_to_all(jnp.broadcast_to(array[None], (size, *array.shape)), axis,...]
    all_to_all x1 -> x0, starting transfers between devices: 4.51 us -> none  [sent_to_all(): lax.all_to_all(jnp.broadcast_to(array[None], (size, *array.shape)), axis,...]
  transfers between devices with their start and end apart: 3 -> 2, of which waited for: 3 -> 2; matrix products, arithmetic and copies ran while one was open for 3% -> 4% of each run, Pallas kernels for 0% -> 0%
where the time goes in v1:
time: 149 us; the launch traced here: 146 us
  Pallas kernels  33.9 us (23%)
  local copies, waits for them, and re-layouts  29.8 us (20%)
  starting transfers between devices  19.7 us (13%)
  matrix products  17.3 us (12%)
  blocking collectives  17.2 us (12%)
  waiting for transfers between devices  16.5 us (11%)
  other arithmetic  9.88 us (7%)
  between operations  1.74 us (1%)
    pallas_call x1, Pallas kernels, grad_sum(): pl.pallas_call(grad_sum_kernel, out_shape=jax.ShapeDtypeStruct((total_row...  33.9 us
    all_to_all x2, starting transfers between devices, surround(): lax.all_to_all(sending, 'space', split_axis=0, concat_axis=0, tiled=True)  19.7 us
    all_to_all x1, blocking collectives, surround(): lax.all_to_all(sending, 'space', split_axis=0, concat_axis=0, tiled=True)  17.2 us
    all_to_all x2, waiting for transfers between devices, surround(): lax.all_to_all(sending, 'space', split_axis=0, concat_axis=0, tiled=True)  16.5 us
    conv_general_dilated x2, matrix products, kernel_grad(): lax.conv_general_dilated(padded[None], grad_block, (dilation, dilation, d...  10.4 us
    broadcast_in_dim x3, other arithmetic, conv_padded(): padded[None]  7.31 us
    conv_general_dilated x2, matrix products, conv_padded(): lax.conv_general_dilated(padded[None], kernel, (1, 1, 1), 'VALID', rhs_di...  6.45 us
    slice x66, local copies, waits for them, and re-layouts, surround(): incoming[tap_index][:, :count_cells]  6.41 us
  transfers between devices with their start and end apart: 2, of which 2 were waited for; matrix products, arithmetic and copies ran while one was open for 4% of the time, Pallas kernels for 0%

profile of v1, /device:TPU:1, one launch (start us, length us, event | category | flops | bytes accessed | tf_op | source)
XLA Modules:
  0.0 146.1 jit_solution(16679912157643508323)
XLA Ops:
  0.6 1.0 copy.719
  1.7 0.7 and_select_fusion.3
  2.4 0.2 dynamic-slice_reduce_fusion
  3.2 0.6 gather_fusion
  3.9 0.3 copy.720
  4.2 0.9 reshape.796
  5.1 13.7 %all-to-all-start = ((bf16[32,2,1536]{2,1,0:T(2,128)(2,1)}), bf16[32,2,1536]{2,1,0:T(2,128)(2,1)S(1)}, u32[]{:S(2)}, u32[]{:S(2)}) async-start(bf16[32,2,1536]{2,1,0:T(2,128)(2,1)} %reshape.796), calls=%async_computation | async-start | bytes 393216 | tf_op jit(solution)/shard_map/all_to_all | solution.py:184
  19.0 0.2 select_reduce_fusion
  19.2 0.2 fusion.22
  19.4 9.4 %all-to-all-done = bf16[32,2,1536]{2,1,0:T(2,128)(2,1)S(1)} async-done(((bf16[32,2,1536]{2,1,0:T(2,128)(2,1)}), bf16[32,2,1536]{2,1,0:T(2,128)(2,1)S(1)}, u32[]{:S(2)}, u32[]{:S(2)}) %all-to-all-start) | async-done | bytes 196640 | tf_op jit(solution)/shard_map/all_to_all | solution.py:184
  28.8 0.3 reshape.797
  29.1 0.6 gather_fusion.1
  32.6 0.3 maximum_bitcast_fusion.2
  32.9 3.1 %fusion.13 = f32[1,48,8,8,8]{1,0,4,3,2:T(1,128)S(1)} fusion(bf16[48,3,3,3,48]{4,0,3,2,1:T(8,128)(2,1)S(1)} %bitcast.751, bf16[1,48,10,10,10]{1,4,3,2,0:T(8,128)(2,1)S(1)} %maximum_bitcast_fusion.2), kind=kOutput, calls=%fused_computation.31 | convolution fusion | flops 63700992 | bytes 318720 | tf_op jit(solution)/shard_map/conv_general_dilated | solution.py:214
  39.2 0.6 gather_fusion.2
  39.8 17.2 %all_to_all.15 = bf16[32,48,128]{2,1,0:T(8,128)(2,1)S(1)} all-to-all(bf16[32,48,128]{2,1,0:T(8,128)(2,1)S(1)} %gather_fusion.2), channel_id=1, replica_groups=mesh['dp'=16,'space'=32] {'space'}, dimensions={0} | all-to-all | bytes 786432 | tf_op jit(solution)/shard_map/all_to_all | solution.py:184
  57.0 0.6 gather_fusion.3
  59.5 0.1 copy.774
  59.7 0.1 copy.791
  59.8 0.1 copy.785
  59.9 0.1 copy.783
  60.0 0.1 copy.782
  60.3 3.4 %maximum_bitcast_fusion = bf16[1,48,12,12,12]{1,4,3,2,0:T(8,128)(2,1)S(1)} fusion(bf16[48,2,2,2]{0,3,2,1:T(2,128)(2,1)S(1)} %bitcast.711, bf16[48,2,2,8]{0,3,2,1:T(8,128)(2,1)S(1)} %bitcast.668, bf16[48,2,2,2]{0,3,2,1:T(2,128)(2,1)S(1)} %bitcast.717, bf16[48,2,8,2]{0,3,2,1:T(2,128)(2,1)S(1)} %bitcast.670, bf16[48,2,8,8]{0,3,2,1:T(8,128)(2,1)S(1)} %bitcast.592, ...), kind=kLoop, calls=%fused_computation.20 | loop fusion | flops 4478976 | bytes 331776 | tf_op jit(solution)/shard_map/broadcast_in_dim | solution.py:215
  63.7 3.4 %fusion.9 = f32[1,48,8,8,8]{1,0,4,3,2:T(1,128)S(1)} fusion(bf16[48,3,3,3,48]{4,0,3,2,1:T(8,128)(2,1)S(1)} %bitcast.562, bf16[1,48,12,12,12]{1,4,3,2,0:T(8,128)(2,1)S(1)} %maximum_bitcast_fusion), kind=kOutput, calls=%fused_computation.18 | convolution fusion | flops 63700992 | bytes 388608 | tf_op jit(solution)/shard_map/conv_general_dilated | solution.py:214
  67.4 0.2 fusion.3
  70.8 1.3 gather_fusion.4
  72.2 6.0 %all-to-all-start.2 = ((bf16[32,48,128]{2,1,0:T(8,128)(2,1)}), bf16[32,48,128]{2,1,0:T(8,128)(2,1)S(1)}, u32[]{:S(2)}, u32[]{:S(2)}) async-start(bf16[32,48,128]{2,1,0:T(8,128)(2,1)} %gather_fusion.4), calls=%async_computation.2 | async-start | bytes 786432 | tf_op jit(solution)/shard_map/all_to_all | solution.py:184
  78.2 3.6 %fusion.7 = f32[48,48,3,3,3]{1,0,4,3,2:T(8,128)S(1)} fusion(bf16[1,48,12,12,12]{1,4,3,2,0:T(8,128)(2,1)S(1)} %maximum_bitcast_fusion, bf16[48,1,8,8,8]{0,4,3,2,1:T(8,128)(2,1)S(1)} %bitcast.573), kind=kOutput, calls=%fused_computation.16 | convolution fusion | flops 63700992 | bytes 463872 | tf_op jit(solution)/shard_map/conv_general_dilated | solution.py:230
  81.8 0.1 fusion.32
  82.0 0.6 copy.862
  82.6 0.7 copy.861
  83.3 0.4 reshape.730
  83.7 7.1 %all-to-all-done.2 = bf16[32,48,128]{2,1,0:T(8,128)(2,1)S(1)} async-done(((bf16[32,48,128]{2,1,0:T(8,128)(2,1)}), bf16[32,48,128]{2,1,0:T(8,128)(2,1)S(1)}, u32[]{:S(2)}, u32[]{:S(2)}) %all-to-all-start.2) | async-done | bytes 393248 | tf_op jit(solution)/shard_map/all_to_all | solution.py:184
  90.8 0.6 gather_fusion.5
  93.3 0.1 copy.832
  94.1 3.6 %maximum_bitcast_fusion.1 = bf16[1,48,12,12,12]{1,4,3,2,0:T(8,128)(2,1)S(1)} fusion(bf16[48,2,2,2]{0,3,2,1:T(2,128)(2,1)S(1)} %bitcast.712, bf16[48,2,2,8]{0,3,2,1:T(8,128)(2,1)S(1)} %bitcast.669, bf16[48,2,2,2]{0,3,2,1:T(2,128)(2,1)S(1)} %bitcast.718, bf16[48,2,8,2]{0,3,2,1:T(2,128)(2,1)S(1)} %bitcast.671, bf16[48,2,8,8]{0,3,2,1:T(8,128)(2,1)S(1)} %bitcast.593, ...), kind=kLoop, calls=%fused_computation.21 | loop fusion | flops 4478976 | bytes 331776 | tf_op jit(solution)/shard_map/broadcast_in_dim | solution.py:215
  97.8 6.8 %fusion.4 = f32[48,48,3,3,3]{1,0,4,3,2:T(8,128)S(1)} fusion(bf16[48,3,3,3,48]{4,0,3,2,1:T(8,128)(2,1)S(1)} %bitcast.563, bf16[1,48,12,12,12]{1,4,3,2,0:T(8,128)(2,1)S(1)} %maximum_bitcast_fusion.1, bf16[1,48,10,10,10]{1,4,3,2,0:T(8,128)(2,1)S(1)} %maximum_bitcast_fusion.2, f32[1,48,8,8,8]{1,0,4,3,2:T(1,128)S(1)} %fusion.13), kind=kOutput, calls=%fused_computation.13 | convolution fusion | flops 127524864 | bytes 733440 | tf_op jit(solution)/shard_map/conv_general_dilated | solution.py:230
  104.6 0.7 copy.857
  105.3 0.4 reshape.727
  105.7 0.8 fusion.11.g_ref
  106.6 33.9 %shard_map.111 = f32[1024,128]{1,0:T(8,128)} custom-call(f32[1024,128]{1,0:T(8,128)} %fusion.11.g_ref), custom_call_target="tpu_custom_call" | custom-call | tf_op jit(solution)/shard_map/pallas_call | solution.py:112
  140.5 1.1 fusion.33
  141.6 0.7 slice.1130
  142.3 0.7 reshape.736
  143.0 0.4 reshape.734
  143.3 1.2 copy.864
  144.6 0.4 reshape.733
  144.9 1.2 copy.863
  (279 shorter events, 14.4 us)
Async XLA Ops:
  0.6 63.1 %copy-start = (bf16[48,27,48]{2,0,1:T(8,128)(2,1)S(1)}, bf16[48,27,48]{2,0,1:T(8,128)(2,1)}, u32[]{:S(2)}) copy-start(bf16[48,27,48]{2,0,1:T(8,128)(2,1)} %param.11) | copy-start | bytes 373252
  3.9 14.9 %copy-start.1 = (s32[27,3]{0,1:T(4,128)S(1)}, s32[27,3]{0,1:T(4,128)}, u32[]{:S(2)}) copy-start(s32[27,3]{0,1:T(4,128)} %constant.93.clone) | copy-start | bytes 976
  3.9 15.1 %copy-start.2 = (s32[1,32]{1,0:T(1,128)S(1)}, s32[1,32]{1,0:T(1,128)}, u32[]{:S(2)}) copy-start(s32[1,32]{1,0:T(1,128)} %param.9) | copy-start | bytes 388
  5.1 23.7 %all-to-all-start = ((bf16[32,2,1536]{2,1,0:T(2,128)(2,1)}), bf16[32,2,1536]{2,1,0:T(2,128)(2,1)S(1)}, u32[]{:S(2)}, u32[]{:S(2)}) async-start(bf16[32,2,1536]{2,1,0:T(2,128)(2,1)} %reshape.796), calls=%async_computation | async-start | bytes 393216 | tf_op jit(solution)/shard_map/all_to_all | solution.py:184
  30.3 2.6 %copy-start.4 = (bf16[48,27,48]{2,0,1:T(8,128)(2,1)S(1)}, bf16[48,27,48]{2,0,1:T(8,128)(2,1)}, u32[]{:S(2)}) copy-start(bf16[48,27,48]{2,0,1:T(8,128)(2,1)} %param.10) | copy-start | bytes 373252
  63.7 3.5 %copy-start.3 = (bf16[3,48]{1,0:T(4,128)(2,1)S(1)}, bf16[3,48]{1,0:T(4,128)(2,1)}, u32[]{:S(2)}) copy-start(bf16[3,48]{1,0:T(4,128)(2,1)} %param.12) | copy-start | bytes 868
  63.7 3.7 %copy-start.5 = (s32[1,1,3,512]{3,1,2,0:T(1,128)S(1)}, s32[1,1,3,512]{3,1,2,0:T(1,128)}, u32[]{:S(2)}) copy-start(s32[1,1,3,512]{3,1,2,0:T(1,128)} %param.13) | copy-start | bytes 18436
  72.2 18.7 %all-to-all-start.2 = ((bf16[32,48,128]{2,1,0:T(8,128)(2,1)}), bf16[32,48,128]{2,1,0:T(8,128)(2,1)S(1)}, u32[]{:S(2)}, u32[]{:S(2)}) async-start(bf16[32,48,128]{2,1,0:T(8,128)(2,1)} %gather_fusion.4), calls=%async_computation.2 | async-start | bytes 786432 | tf_op jit(solution)/shard_map/all_to_all | solution.py:184

commit v2 on v1

v2 whole, which is shorter than its diff:
```python
import functools
import jax
import jax.numpy as jnp
from jax import lax
from jax.experimental import pallas as pl
from jax.experimental.pallas import tpu as pltpu
from jax.sharding import PartitionSpec as P

BF = jnp.bfloat16
F32 = jnp.float32
C = 48
LANES = 256
NT = (((1,), (1,)), ((), ()))


def dot32(a, b):
    return jnp.dot(a, b, preferred_element_type=F32)


def elu_pair(values):
    negative = jnp.exp(jnp.minimum(values, 0.0))
    return (jnp.where(values > 0, values, negative - 1.0), jnp.where(values > 0, 1.0, negative))


def plane(index):
    start = index * LANES
    return pl.ds(start if isinstance(index, int) else pl.multiple_of(start, LANES), LANES)


def compute_kernel(scale, ids_ref, got_ref, w1_ref, w2_ref, wb_ref, head_ref, head_t_ref,
                   logits_ref, grads_ref,
                   table, near, near_t, wide1, out1, pre1, wide2, out2, wide_b, out_b, lhs2, lhs1, want, mask_ref,
                   head_acc):
    me = lax.axis_index("space")

    @pl.loop(0, 64)
    def _(i):
        table[i] = -1

    @pl.loop(0, 32)
    def _(j):
        table[ids_ref[0, j]] = j

    own = ids_ref[0, me]
    ox, oy, oz = own // 16, own // 4 % 4, own % 4
    slots, present = [], []
    for t in range(27):
        x, y, z = ox + t // 9 - 1, oy + t // 3 % 3 - 1, oz + t % 3 - 1
        inside = (x >= 0) & (x < 4) & (y >= 0) & (y < 4) & (z >= 0) & (z < 4)
        found = table[jnp.where(inside, (x * 4 + y) * 4 + z, own)]
        ok = inside & (found >= 0)
        slots.append(jnp.where(ok, found, me))
        present.append(jnp.where(ok, 1.0, 0.0).astype(F32))

    low_half = lax.broadcasted_iota(jnp.int32, (C, 128), 1) < 64

    def tiles_of(bx, row, rows):
        return [
            (got_ref[slots[bx * 9 + j], row:row + rows, :].astype(F32) * present[bx * 9 + j]).astype(BF)
            for j in range(9)
        ]

    def face_tiles(tiles, half):
        rows = tiles[0].shape[0]
        keep = low_half[:rows]
        flip = lambda v: pltpu.roll(v, 64, 1)
        for k in range(5):
            low = tiles[2 * k] if half == 0 else flip(tiles[2 * k])
            if k == 4:
                high = jnp.zeros_like(low)
            else:
                high = tiles[2 * k + 1] if half == 1 else flip(tiles[2 * k + 1])
            yield k, jnp.where(keep, low, high)

    for bx in range(3):
        for pair in range(4):
            spots = [(half, bx * 8 + pair * 2 + half - 3) for half in range(2)]
            spots = [(half, at) for half, at in spots if 0 <= at < 18]
            if not spots:
                continue
            tiles = tiles_of(bx, pair * C, C)
            for half, at in spots:
                for k, value in face_tiles(tiles, half):
                    near[at * C:(at + 1) * C, k * 128:(k + 1) * 128] = value
        tiles = tiles_of(bx, 4 * C, 16)
        for half in range(2):
            for k, value in face_tiles(tiles, half):
                near_t[(bx * 2 + half) * 16:(bx * 2 + half + 1) * 16, k * 128:(k + 1) * 128] = value

    lane = lax.broadcasted_iota(jnp.int32, (1, LANES), 1)
    face_row = lax.broadcasted_iota(jnp.int32, (640, LANES), 0)

    def select_of(b, c):
        y = (lane >> 4) + (b + 3)
        z = (lane & 15) + (c + 3)
        source = ((y >> 3) * 3 + (z >> 3)) * 64 + (y & 7) * 8 + (z & 7)
        return jnp.where(face_row == source, 1.0, 0.0).astype(BF)

    @pl.loop(0, 9)
    def _(bc):
        picked = dot32(near[...], select_of(bc // 3, bc % 3)).astype(BF)
        rows = pl.ds(pl.multiple_of(bc * C, 16), C)
        for at in range(18):
            wide1[rows, plane(at)] = picked[at * C:(at + 1) * C]

    picked_t = dot32(near_t[...], select_of(1, 1))
    want[...] = jnp.zeros_like(want)
    for xo in range(2, 14):
        bx, x = (xo + 4) // 8, (xo + 4) % 8
        row = (bx * 2 + x % 2) * 16 + (x // 2) * 4
        want[xo - 2, 0:3, :] = picked_t[row:row + 3]

    y, z = lane >> 4, lane & 15
    region = ((y + 4) >> 3) * 3 + ((z + 4) >> 3)
    inner = jnp.where((y >= 2) & (y < 14) & (z >= 2) & (z < 14), 1.0, 0.0)
    own_lane = jnp.where((y >= 4) & (y < 12) & (z >= 4) & (z < 12), 1.0, 0.0)
    for bx in range(3):
        row = jnp.zeros((1, LANES), F32)
        for j in range(9):
            row = jnp.where(region == j, present[bx * 9 + j], row)
        mask_ref[bx, 0:1, :] = row
        mask_ref[bx, 1:2, :] = row * inner

    def region_of(xo):
        return jnp.where(xo >= 12, 2, jnp.where(xo >= 4, 1, 0))

    out1[...] = dot32(w1_ref[...], wide1[...])

    @pl.loop(0, 16)
    def _(xo):
        pre = out1[0:C, plane(xo)] + out1[C:2 * C, plane(xo + 1)] + out1[2 * C:3 * C, plane(xo + 2)]
        pre1[xo] = pre
        act, _slope = elu_pair(pre)
        hid = (act * mask_ref[region_of(xo), 0:1, :]).astype(BF)
        for bc in range(9):
            shift = -(32 * (bc // 3 - 1) + 2 * (bc % 3 - 1)) % LANES
            wide2[bc * C:(bc + 1) * C, plane(xo)] = pltpu.roll(hid, shift, 1) if shift else hid

    out2[...] = dot32(w2_ref[...], wide2[...])
    lhs2[...] = jnp.zeros_like(lhs2)
    lhs1[...] = jnp.zeros_like(lhs1)
    head_acc[...] = jnp.zeros_like(head_acc)

    def second(xo, is_own):
        pre = out2[0:C, plane(xo - 2)] + out2[C:2 * C, plane(xo)] + out2[2 * C:3 * C, plane(xo + 2)]
        act, slope = elu_pair(pre)
        mask = mask_ref[region_of(xo), 1:2, :]
        hid = (act * mask).astype(BF)
        logits = dot32(head_ref[...], hid)
        grad_logit = ((jax.nn.sigmoid(logits) - want[xo - 2]) * mask * scale).astype(BF)
        back = dot32(head_t_ref[...], grad_logit)
        grad_pre = (back * slope * mask).astype(BF)
        for bc in range(9):
            shift = (32 * (bc // 3 - 1) + 2 * (bc % 3 - 1)) % LANES
            wide_b[bc * C:(bc + 1) * C, plane(xo - 2)] = pltpu.roll(grad_pre, shift, 1) if shift else grad_pre
        if is_own:
            logits_ref[xo - 4] = logits[0:8]
            own_logit = (grad_logit.astype(F32) * own_lane).astype(BF)
            head_acc[...] += lax.dot_general(own_logit, hid, NT, preferred_element_type=F32)
            own_pre = (grad_pre.astype(F32) * own_lane).astype(BF)
            for a in range(3):
                lhs2[a * C:(a + 1) * C, plane(xo + 2 * a - 4)] = own_pre

    @pl.loop(0, 8)
    def _(i):
        second(i + 4, True)

    @pl.loop(0, 4)
    def _(i):
        second(jnp.where(i < 2, i + 2, i + 10), False)

    grads_ref[3 * C:6 * C, 0:9 * C] = lax.dot_general(
        lhs2[...], wide2[:, 2 * LANES:14 * LANES], NT, preferred_element_type=F32)
    out_b[...] = dot32(wb_ref[...], wide_b[...])

    @pl.loop(4, 12)
    def _(q):
        back = out_b[0:C, plane(q)] + out_b[C:2 * C, plane(q - 2)] + out_b[2 * C:3 * C, plane(q - 4)]
        _act, slope = elu_pair(pre1[q])
        grad_pre = (back * slope * own_lane).astype(BF)
        for a in range(3):
            lhs1[a * C:(a + 1) * C, plane(q + a - 4)] = grad_pre

    grads_ref[0:3 * C, 0:9 * C] = lax.dot_general(
        lhs1[...], wide1[:, 4 * LANES:14 * LANES], NT, preferred_element_type=F32)
    grads_ref[:, 9 * C:512] = jnp.zeros((6 * C, 512 - 9 * C), F32)
    grads_ref[0:16, 9 * C:10 * C] = head_acc[...]


def compute_block(ids, got, w1, w2, wb, head, head_t, scale):
    vmem = pl.BlockSpec(memory_space=pltpu.VMEM)
    v = pltpu.VMEM
    return pl.pallas_call(
        functools.partial(compute_kernel, scale),
        out_shape=(jax.ShapeDtypeStruct((8, 8, LANES), F32), jax.ShapeDtypeStruct((6 * C, 512), F32)),
        in_specs=[pl.BlockSpec(memory_space=pltpu.SMEM)] + [vmem] * 6,
        out_specs=(vmem, vmem),
        scratch_shapes=[
            pltpu.SMEM((64,), jnp.int32),
            v((18 * C, 640), BF), v((96, 640), BF),
            v((9 * C, 18 * LANES), BF), v((3 * C, 18 * LANES), F32), v((16, C, LANES), F32),
            v((9 * C, 16 * LANES), BF), v((3 * C, 16 * LANES), F32),
            v((9 * C, 12 * LANES), BF), v((3 * C, 12 * LANES), F32),
            v((3 * C, 12 * LANES), BF), v((3 * C, 10 * LANES), BF),
            v((12, 16, LANES), F32), v((3, 8, LANES), F32), v((16, C), F32),
        ],
        compiler_params=pltpu.CompilerParams(vmem_limit_bytes=60 * 1024 * 1024),
    )(ids, got, w1, w2, wb, head, head_t)


def stacked(kernel):
    return kernel.reshape(C, 3, 9 * C).transpose(1, 0, 2).reshape(3 * C, 9 * C)


def stacked_back(kernel):
    return kernel.reshape(C, 3, 9, C).transpose(1, 3, 2, 0).reshape(3 * C, 9 * C)


def payload(features, targets):
    feats = features.reshape(C, 4, 128).transpose(1, 0, 2).reshape(4 * C, 128)
    wants = jnp.pad(targets.astype(BF).reshape(3, 4, 128).transpose(1, 0, 2), ((0, 0), (0, 1), (0, 0)))
    return jnp.concatenate([feats, wants.reshape(16, 128)], axis=0)


MESH = pl.DeviceIdType.MESH
N_Z, N_X = 8, 4
SPLIT = 96


def gather_kernel(own_ref, got_ref, send_sem, recv_sem):
    dp, sp = lax.axis_index("dp"), lax.axis_index("space")
    z, x = lax.div(sp, N_X), lax.rem(sp, N_X)

    def at(dz, dx):
        return lax.rem(z + dz + N_Z, N_Z) * N_X + lax.rem(x + dx + N_X, N_X)

    near_by = [(1, 0), (-1, 0), (0, 1), (0, -1), (0, 2)]
    barrier = pltpu.get_barrier_semaphore()
    for dz, dx in near_by:
        pl.semaphore_signal(barrier, inc=1, device_id=(dp, at(dz, dx)), device_id_type=MESH)
    pl.semaphore_wait(barrier, len(near_by))

    rows = [pl.ds(0, SPLIT), pl.ds(SPLIT, own_ref.shape[0] - SPLIT)]
    sent = []

    def copy(half, dz, dx, to, number):
        slot = at(dz, dx)
        source = own_ref.at[rows[half]] if (dz, dx) == (0, 0) else got_ref.at[slot, rows[half]]
        return pltpu.make_async_remote_copy(
            src_ref=source, dst_ref=got_ref.at[slot, rows[half]], send_sem=send_sem.at[number],
            recv_sem=recv_sem.at[half, slot], device_id=(dp, at(*to)), device_id_type=MESH)

    def send(half, dz, dx, to):
        one = copy(half, dz, dx, to, len(sent))
        one.start()
        sent.append(one)

    arrived = set()

    def await_block(half, dz, dx):
        if (half, dz, dx) not in arrived and (dz, dx) != (0, 0):
            slot = at(dz, dx)
            pltpu.make_async_remote_copy(
                src_ref=own_ref.at[rows[half]], dst_ref=got_ref.at[slot, rows[half]], send_sem=send_sem.at[0],
                recv_sem=recv_sem.at[half, slot], device_id=(dp, at(0, 1)), device_id_type=MESH).wait_recv()
            arrived.add((half, dz, dx))

    def reach(way, dx):
        return 4 if (way == 1) == (dx in (0, 1)) else 3

    for way in (1, -1):
        send(1, 0, 0, (way, 0))
    for dx in (1, -1, 2):
        send(0, 0, 0, (0, dx))
    for way in (1, -1):
        send(0, 0, 0, (way, 0))
    for dx in (1, -1, 2):
        send(1, 0, 0, (0, dx))
    got_ref[sp] = own_ref[...]

    for k in range(4):
        for dx in (0, 1, -1, 2):
            for way in (1, -1):
                if (k, dx) != (0, 0) and k < reach(way, dx):
                    await_block(0, -way * k, dx)
                    send(0, -way * k, dx, (way, 0))
        for way in (1, -1):
            far = k + 1
            if far <= reach(way, 0):
                await_block(1, -way * far, 0)
                if far < reach(way, 0):
                    send(1, -way * far, 0, (way, 0))
                for dx in (1, -1, 2):
                    send(1, -way * far, 0, (0, dx))

    for half in range(2):
        for dx in (0, 1, -1, 2):
            column = dx if half == 0 else 0
            for way in (1, -1):
                for k in range(reach(way, column) + 1):
                    await_block(half, -way * k, dx)
    for one in sent:
        one.wait_send()


def gather_blocks(own):
    vmem = pl.BlockSpec(memory_space=pltpu.VMEM)
    return pl.pallas_call(
        gather_kernel,
        out_shape=jax.ShapeDtypeStruct((N_Z * N_X, *own.shape), own.dtype),
        in_specs=[vmem],
        out_specs=vmem,
        scratch_shapes=[pltpu.SemaphoreType.DMA((64,)), pltpu.SemaphoreType.DMA((2, N_Z * N_X))],
        compiler_params=pltpu.CompilerParams(collective_id=1, has_side_effects=True),
    )(own)


def grad_sum_kernel(g_ref, out_ref, send_buf, rs_buf, dp_buf, ag_buf, send_sem, rs_sem, dp_send, dp_sem, ag_send, ag_sem):
    dp, sp = lax.axis_index("dp"), lax.axis_index("space")
    n_dp, n_sp = dp_buf.shape[0], rs_buf.shape[0]
    rows = rs_buf.shape[1]

    barrier = pltpu.get_barrier_semaphore()

    @pl.loop(1, n_sp)
    def _(r):
        pl.semaphore_signal(barrier, inc=1, device_id=(dp, lax.rem(sp + r, n_sp)), device_id_type=MESH)

    @pl.loop(1, n_dp)
    def _(r):
        pl.semaphore_signal(barrier, inc=1, device_id=(lax.rem(dp + r, n_dp), sp), device_id_type=MESH)

    send_buf[...] = g_ref[...].astype(jnp.bfloat16)
    pl.semaphore_wait(barrier, n_sp + n_dp - 2)

    def rs_copy(r):
        peer = lax.rem(sp + r, n_sp)
        return pltpu.make_async_remote_copy(
            src_ref=send_buf.at[peer], dst_ref=rs_buf.at[r], send_sem=send_sem.at[r], recv_sem=rs_sem.at[r],
            device_id=(dp, peer), device_id_type=MESH)

    def dp_copy(r):
        peer = lax.rem(dp + r, n_dp)
        return pltpu.make_async_remote_copy(
            src_ref=dp_buf.at[0], dst_ref=dp_buf.at[r], send_sem=dp_send.at[r], recv_sem=dp_sem.at[r],
            device_id=(peer, sp), device_id_type=MESH)

    def ag_copy(r):
        peer = lax.rem(sp + r, n_sp)
        return pltpu.make_async_remote_copy(
            src_ref=ag_buf.at[0], dst_ref=ag_buf.at[r], send_sem=ag_send.at[r], recv_sem=ag_sem.at[r],
            device_id=(dp, peer), device_id_type=MESH)

    @pl.loop(1, n_sp)
    def _(r):
        rs_copy(r).start()

    def add_rs(r, total):
        rs_copy(r).wait_recv()
        return total + rs_buf[r].astype(jnp.float32)

    own = g_ref[sp]
    total = lax.fori_loop(1, n_sp, add_rs, own)
    dp_buf[0] = total.astype(jnp.bfloat16)

    @pl.loop(1, n_dp)
    def _(r):
        dp_copy(r).start()

    @pl.loop(1, n_dp)
    def _(r):
        dp_copy(r).wait_recv()

    def add_dp(d, total):
        return total + dp_buf[lax.rem(dp - d + n_dp, n_dp)].astype(jnp.float32)

    total = lax.fori_loop(0, n_dp, add_dp, jnp.zeros((rows, 128), jnp.float32))
    ag_buf[0] = total.astype(jnp.bfloat16)

    @pl.loop(1, n_sp)
    def _(r):
        ag_copy(r).start()

    @pl.loop(1, n_sp)
    def _(r):
        rs_copy(r).wait_send()

    @pl.loop(1, n_dp)
    def _(r):
        dp_copy(r).wait_send()

    out_ref[sp] = ag_buf[0].astype(jnp.float32)

    @pl.loop(1, n_sp)
    def _(r):
        ag_copy(r).wait_recv()
        source = lax.rem(sp - r + n_sp, n_sp)
        out_ref[source] = ag_buf[r].astype(jnp.float32)

    @pl.loop(1, n_sp)
    def _(r):
        ag_copy(r).wait_send()


def grad_sum(flat):
    n_dp, n_sp = lax.axis_size("dp"), lax.axis_size("space")
    rows = flat.shape[1]
    vmem = pl.BlockSpec(memory_space=pltpu.VMEM)
    dma = pltpu.SemaphoreType.DMA
    return pl.pallas_call(
        grad_sum_kernel,
        out_shape=jax.ShapeDtypeStruct(flat.shape, jnp.float32),
        in_specs=[vmem],
        out_specs=vmem,
        scratch_shapes=[
            pltpu.VMEM((n_sp, rows, 128), jnp.bfloat16),
            pltpu.VMEM((n_sp, rows, 128), jnp.bfloat16),
            pltpu.VMEM((n_dp, rows, 128), jnp.bfloat16),
            pltpu.VMEM((n_sp, rows, 128), jnp.bfloat16),
            dma((n_sp,)), dma((n_sp,)), dma((n_dp,)), dma((n_dp,)), dma((n_sp,)), dma((n_sp,)),
        ],
        compiler_params=pltpu.CompilerParams(collective_id=0, has_side_effects=True),
    )(flat)


def on_device(features, device_block, conv_first, conv_second, head_weight, targets):
    n_dp, n_sp = lax.axis_size("dp"), lax.axis_size("space")
    scale = (n_dp * n_sp * 3 * 512) ** (-0.5)
    got = gather_blocks(payload(features[0, 0], targets[0, 0]))
    head = jnp.pad(head_weight, ((0, 13), (0, 0)))
    logits, grads = compute_block(
        device_block, got, stacked(conv_first), stacked(conv_second), stacked_back(conv_second), head, head.T, scale)
    logits = logits[:, :3].reshape(8, 3, 16, 16)[:, :, 4:12, 4:12].transpose(1, 0, 2, 3).reshape(3, 512)
    tiles = grads.reshape(6, C, 4, 128).transpose(0, 2, 1, 3).reshape(24, C, 128)
    tiles = grad_sum(jnp.pad(tiles, ((0, n_sp - 24), (0, 0), (0, 0))))[:24]
    grads = tiles.reshape(2, 3, 4, C, 128).transpose(0, 3, 1, 2, 4).reshape(2, C, 3, 512)
    kernels = grads[..., :9 * C].reshape(2, C, 27, C)
    return (logits[None, None], kernels[0], kernels[1], grads[0, :3, 0, 9 * C:10 * C])


def solution(mesh):
    in_specs = (
        P("dp", "space", None, None),
        P("dp", None),
        P(),
        P(),
        P(),
        P("dp", "space", None, None),
    )
    out_specs = (P("dp", "space", None, None), P(), P(), P())
    return jax.shard_map(
        on_device, mesh=mesh, in_specs=in_specs, out_specs=out_specs, check_vma=False
    )
```

time: 149 us -> 113 us (0.76); the launches traced: 146 us -> 112 us
  Pallas kernels: 33.9 us -> 92.5 us
  starting transfers between devices: 19.7 us -> 0 us
  matrix products: 17.3 us -> 0 us
  blocking collectives: 17.2 us -> 0 us
  waiting for transfers between devices: 16.5 us -> 0 us
  local copies, waits for them, and re-layouts: 29.8 us -> 17.3 us
  other arithmetic: 9.88 us -> 1.39 us
    pallas_call x1 -> x3, Pallas kernels: 33.9 us -> 92.5 us  [the longest x1 42.4 us: grad_sum(): pl.pallas_call(grad_sum_kernel, out_shape=jax.ShapeDtypeStruct(flat.shape...]
    all_to_all x2 -> x0, starting transfers between devices: 19.7 us -> none  [surround(): lax.all_to_all(sending, 'space', split_axis=0, concat_axis=0, tiled=True)]
    all_to_all x1 -> x0, blocking collectives: 17.2 us -> none  [surround(): lax.all_to_all(sending, 'space', split_axis=0, concat_axis=0, tiled=True)]
    conv_general_dilated x4 -> x0, matrix products: 16.9 us -> none  [the longest x2 10.4 us: kernel_grad(): lax.conv_general_dilated(padded[None], grad_block, (dilation, dilation, d...]
    all_to_all x2 -> x0, waiting for transfers between devices: 16.5 us -> none  [surround(): lax.all_to_all(sending, 'space', split_axis=0, concat_axis=0, tiled=True)]
    broadcast_in_dim x3 -> x0, other arithmetic: 7.31 us -> none  [conv_padded(): padded[None]]
    slice x85 -> x6, local copies, waits for them, and re-layouts: 8.54 us -> 2.41 us  [the longest x1 1.1 us: on_device(): tiles = grad_sum(jnp.pad(tiles, ((0, n_sp - 24), (0, 0), (0, 0))))[:24]]
    reshape x74 -> x9, local copies, waits for them, and re-layouts: 8.5 us -> 3.51 us  [the longest x2 1.29 us: on_device(): grads.reshape(6, C, 4, 128).transpose(0, 2, 1, 3).reshape(24, C, 128)]
  transfers between devices with their start and end apart: 2 -> 0, of which waited for: 2 -> 0; matrix products, arithmetic and copies ran while one was open for 4% -> 0% of each run, Pallas kernels for 0% -> 0%
where the time goes in v2:
time: 113 us; the launch traced here: 112 us
  Pallas kernels  92.5 us (82%)
  local copies, waits for them, and re-layouts  17.3 us (15%)
  other arithmetic  1.39 us (1%)
    pallas_call x1, Pallas kernels, grad_sum(): pl.pallas_call(grad_sum_kernel, out_shape=jax.ShapeDtypeStruct(flat.shape...  42.4 us
    pallas_call x1, Pallas kernels, gather_blocks(): pl.pallas_call(gather_kernel, out_shape=jax.ShapeDtypeStruct((N_Z * N_X,...  30.5 us
    pallas_call x1, Pallas kernels, compute_block(): pl.pallas_call(functools.partial(compute_kernel, scale), out_shape=(jax.S...  19.7 us
    unnamed x8, local copies, waits for them, and re-layouts  4.5 us

profile of v2, /device:TPU:1, one launch (start us, length us, event | category | flops | bytes accessed | tf_op | source)
XLA Modules:
  0.0 112.0 jit_solution(15330621547585100914)
XLA Ops:
  0.6 0.0 copy-start
  0.6 0.8 convert_reduce_fusion
  1.4 0.8 copy.43
  2.2 0.1 copy.57
  2.3 0.6 pad_bitcast_fusion.head_t_ref
  2.9 0.6 pad.13.clone.head_ref
  3.5 0.8 reshape_squeeze.3
  4.3 0.6 pad_maximum_fusion.own_ref
  5.0 1.1 copy.38
  6.0 0.4 reshape.57
  6.5 0.7 copy.39
  7.2 0.0 copy-done
  7.2 0.1 copy.40
  7.3 0.4 reshape.59
  7.7 0.7 copy.41
  8.4 0.2 copy.59
  8.6 0.2 reshape.62
  8.8 0.8 copy.44.wb_ref
  9.6 30.5 %shard_map.93.got_ref = bf16[32,208,128]{2,1,0:T(8,128)(2,1)} custom-call(bf16[208,128]{1,0:T(8,128)(2,1)} %pad_maximum_fusion.own_ref), custom_call_target="tpu_custom_call" | custom-call | tf_op jit(solution)/shard_map/pallas_call | solution.py:308
  40.1 19.7 %shard_map.94 = (f32[8,8,256]{2,1,0:T(8,128)}, f32[288,512]{1,0:T(8,128)}) custom-call(s32[1,32]{1,0:T(1,128)} %ids_ref.1, bf16[32,208,128]{2,1,0:T(8,128)(2,1)} %shard_map.93.got_ref, bf16[144,432]{1,0:T(8,128)(2,1)} %bitcast.47, bf16[144,432]{1,0:T(8,128)(2,1)} %bitcast.48, bf16[144,432]{1,0:T(8,128)(2,1)} %copy.44.wb_ref, ...), custom_call_target="tpu_custom_call" | custom-call | tf_op jit(solution)/shard_map/pallas_call | solution.py:193
  59.8 0.8 slice.23
  60.6 0.1 reshape.63
  60.7 0.1 slice_bitcast_fusion
  60.8 0.7 broadcast_in_dim_reshape.4
  61.5 1.3 %reshape.64 = f32[6,48,4,128]{3,2,1,0:T(4,128)S(1)} reshape(f32[288,512]{1,0:T(8,128)} %get-tuple-element.7) | data formatting | bytes 1179648 | tf_op jit(solution)/shard_map/reshape | solution.py:434
  62.8 0.9 pad.14.g_ref
  63.8 42.4 %shard_map.95 = f32[32,48,128]{2,1,0:T(8,128)} custom-call(f32[32,48,128]{2,1,0:T(8,128)} %pad.14.g_ref), custom_call_target="tpu_custom_call" | custom-call | tf_op jit(solution)/shard_map/pallas_call | solution.py:410
  106.2 1.1 slice.25
  107.3 0.1 copy.58
  107.3 0.7 slice_bitcast_fusion.1
  108.0 0.2 copy.50
  108.3 0.5 squeeze.11
  108.8 1.2 %copy.53 = f32[48,27,48]{2,0,1:T(8,128)} copy(f32[48,27,48]{2,1,0:T(8,128)S(1)} %squeeze.11) | data formatting | bytes 497664
  110.0 0.2 copy.49
  110.2 0.5 squeeze.10
  110.8 1.2 %copy.52 = f32[48,27,48]{2,0,1:T(8,128)} copy(f32[48,27,48]{2,1,0:T(8,128)S(1)} %squeeze.10) | data formatting | bytes 497664
  (5 shorter events, 0.1 us)
Async XLA Ops:
  0.6 6.5 %copy-start = (bf16[48,27,48]{2,0,1:T(8,128)(2,1)S(1)}, bf16[48,27,48]{2,0,1:T(8,128)(2,1)}, u32[]{:S(2)}) copy-start(bf16[48,27,48]{2,0,1:T(8,128)(2,1)} %param.9) | copy-start | bytes 373252

commit v3 on v2

--- a/solution.py
+++ b/solution.py
@@ -11,6 +11,7 @@
 C = 48
 LANES = 256
 NT = (((1,), (1,)), ((), ()))
+TN = (((0,), (0,)), ((), ()))
 
 
 def dot32(a, b):
@@ -27,11 +28,30 @@
     return pl.ds(start if isinstance(index, int) else pl.multiple_of(start, LANES), LANES)
 
 
-def compute_kernel(scale, ids_ref, got_ref, w1_ref, w2_ref, wb_ref, head_ref, head_t_ref,
+def pack_grads(grads_ref, part, grads, head):
+    for group in range(9):
+        rows = grads[group * 16:(group + 1) * 16]
+        for col in range(3):
+            grads_ref[part, group * 3 + col] = rows[:, col * 128:(col + 1) * 128]
+        grads_ref[part, 27 + group // 2, :, 64 * (group % 2):64 * (group % 2) + C] = rows[:, 384:9 * C]
+    grads_ref[part, 31, :, 64:64 + C] = head
+
+
+def compute_kernel(scale, ids_ref, got_ref, k1_ref, k2_ref, head_in_ref,
                    logits_ref, grads_ref,
                    table, near, near_t, wide1, out1, pre1, wide2, out2, wide_b, out_b, lhs2, lhs1, want, mask_ref,
-                   head_acc):
+                   head_acc, w1_ref, w2_ref, wb_ref, head_ref, raw_logits):
     me = lax.axis_index("space")
+
+    for t in range(27):
+        a, bc = t // 9, t % 9
+        w1_ref[a * C:(a + 1) * C, bc * C:(bc + 1) * C] = k1_ref[t]
+        w2_ref[a * C:(a + 1) * C, bc * C:(bc + 1) * C] = k2_ref[t]
+        wb_ref[bc * C:(bc + 1) * C, a * C:(a + 1) * C] = k2_ref[t]
+    head_ref[...] = jnp.zeros_like(head_ref)
+    head_ref[0:3, :] = head_in_ref[...].astype(F32)
+    head = head_ref[...].astype(BF)
+    head_t = head_ref[...].T.astype(BF)
 
     @pl.loop(0, 64)
     def _(i):
@@ -146,15 +166,15 @@
         act, slope = elu_pair(pre)
         mask = mask_ref[region_of(xo), 1:2, :]
         hid = (act * mask).astype(BF)
-        logits = dot32(head_ref[...], hid)
+        logits = dot32(head, hid)
         grad_logit = ((jax.nn.sigmoid(logits) - want[xo - 2]) * mask * scale).astype(BF)
-        back = dot32(head_t_ref[...], grad_logit)
+        back = dot32(head_t, grad_logit)
         grad_pre = (back * slope * mask).astype(BF)
         for bc in range(9):
             shift = (32 * (bc // 3 - 1) + 2 * (bc % 3 - 1)) % LANES
             wide_b[bc * C:(bc + 1) * C, plane(xo - 2)] = pltpu.roll(grad_pre, shift, 1) if shift else grad_pre
         if is_own:
-            logits_ref[xo - 4] = logits[0:8]
+            raw_logits[pl.ds(pl.multiple_of((xo - 4) * 8, 8), 8), :] = logits[0:8]
             own_logit = (grad_logit.astype(F32) * own_lane).astype(BF)
             head_acc[...] += lax.dot_general(own_logit, hid, NT, preferred_element_type=F32)
             own_pre = (grad_pre.astype(F32) * own_lane).astype(BF)
@@ -169,9 +189,10 @@
     def _(i):
         second(jnp.where(i < 2, i + 2, i + 10), False)
 
-    grads_ref[3 * C:6 * C, 0:9 * C] = lax.dot_general(
-        lhs2[...], wide2[:, 2 * LANES:14 * LANES], NT, preferred_element_type=F32)
-    out_b[...] = dot32(wb_ref[...], wide_b[...])
+    grads_ref[:, 27:32] = jnp.zeros((2, 5, 16, 128), F32)
+    pack_grads(grads_ref, 1, lax.dot_general(
+        lhs2[...], wide2[:, 2 * LANES:14 * LANES], NT, preferred_element_type=F32), jnp.zeros((16, C), F32))
+    out_b[...] = lax.dot_general(wb_ref[...], wide_b[...], TN, preferred_element_type=F32)
 
     @pl.loop(4, 12)
     def _(q):
@@ -181,19 +202,29 @@
         for a in range(3):
             lhs1[a * C:(a + 1) * C, plane(q + a - 4)] = grad_pre
 
-    grads_ref[0:3 * C, 0:9 * C] = lax.dot_general(
-        lhs1[...], wide1[:, 4 * LANES:14 * LANES], NT, preferred_element_type=F32)
-    grads_ref[:, 9 * C:512] = jnp.zeros((6 * C, 512 - 9 * C), F32)
-    grads_ref[0:16, 9 * C:10 * C] = head_acc[...]
-
-
-def compute_block(ids, got, w1, w2, wb, head, head_t, scale):
+    pack_grads(grads_ref, 0, lax.dot_general(
+        lhs1[...], wide1[:, 4 * LANES:14 * LANES], NT, preferred_element_type=F32), head_acc[...])
+
+    high = raw_logits[...].astype(BF)
+    rest = raw_logits[...] - high.astype(F32)
+    middle = rest.astype(BF)
+    low = (rest - middle.astype(F32)).astype(BF)
+    cell = lax.broadcasted_iota(jnp.int32, (1, 64), 1)
+    source = ((cell >> 3) + 4) * 16 + (cell & 7) + 4
+    pick = jnp.where(lax.broadcasted_iota(jnp.int32, (LANES, 64), 0) == source, 1.0, 0.0).astype(BF)
+    parts = dot32(jnp.concatenate([high, middle, low], axis=0), pick)
+    own_logits = (parts[0:64] + parts[64:128]) + parts[128:192]
+    for x in range(8):
+        logits_ref[:, x * 64:(x + 1) * 64] = own_logits[x * 8:x * 8 + 3]
+
+
+def compute_block(ids, got, k1, k2, head, scale):
     vmem = pl.BlockSpec(memory_space=pltpu.VMEM)
     v = pltpu.VMEM
     return pl.pallas_call(
         functools.partial(compute_kernel, scale),
-        out_shape=(jax.ShapeDtypeStruct((8, 8, LANES), F32), jax.ShapeDtypeStruct((6 * C, 512), F32)),
-        in_specs=[pl.BlockSpec(memory_space=pltpu.SMEM)] + [vmem] * 6,
+        out_shape=(jax.ShapeDtypeStruct((3, 512), F32), jax.ShapeDtypeStruct((2, 32, 16, 128), F32)),
+        in_specs=[pl.BlockSpec(memory_space=pltpu.SMEM)] + [vmem] * 4,
         out_specs=(vmem, vmem),
         scratch_shapes=[
             pltpu.SMEM((64,), jnp.int32),
@@ -203,23 +234,11 @@
             v((9 * C, 12 * LANES), BF), v((3 * C, 12 * LANES), F32),
             v((3 * C, 12 * LANES), BF), v((3 * C, 10 * LANES), BF),
             v((12, 16, LANES), F32), v((3, 8, LANES), F32), v((16, C), F32),
+            v((3 * C, 9 * C), BF), v((3 * C, 9 * C), BF), v((9 * C, 3 * C), BF), v((16, C), F32),
+            v((64, LANES), F32),
         ],
         compiler_params=pltpu.CompilerParams(vmem_limit_bytes=60 * 1024 * 1024),
-    )(ids, got, w1, w2, wb, head, head_t)
-
-
-def stacked(kernel):
-    return kernel.reshape(C, 3, 9 * C).transpose(1, 0, 2).reshape(3 * C, 9 * C)
-
-
-def stacked_back(kernel):
-    return kernel.reshape(C, 3, 9, C).transpose(1, 3, 2, 0).reshape(3 * C, 9 * C)
-
-
-def payload(features, targets):
-    feats = features.reshape(C, 4, 128).transpose(1, 0, 2).reshape(4 * C, 128)
-    wants = jnp.pad(targets.astype(BF).reshape(3, 4, 128).transpose(1, 0, 2), ((0, 0), (0, 1), (0, 0)))
-    return jnp.concatenate([feats, wants.reshape(16, 128)], axis=0)
+    )(ids, got, k1, k2, head)
 
 
 MESH = pl.DeviceIdType.MESH
@@ -227,7 +246,7 @@
 SPLIT = 96
 
 
-def gather_kernel(own_ref, got_ref, send_sem, recv_sem):
+def gather_kernel(features_ref, targets_ref, got_ref, own_ref, wants, send_sem, recv_sem):
     dp, sp = lax.axis_index("dp"), lax.axis_index("space")
     z, x = lax.div(sp, N_X), lax.rem(sp, N_X)
 
@@ -238,6 +257,14 @@
     barrier = pltpu.get_barrier_semaphore()
     for dz, dx in near_by:
         pl.semaphore_signal(barrier, inc=1, device_id=(dp, at(dz, dx)), device_id_type=MESH)
+
+    wants[...] = jnp.zeros_like(wants)
+    for pair in range(4):
+        lanes = slice(pair * 128, (pair + 1) * 128)
+        own_ref[pair * C:(pair + 1) * C, :] = features_ref[0, 0, :, lanes]
+        wants[pair * 4:pair * 4 + 3, :] = targets_ref[0, 0, :, lanes].astype(F32)
+    own_ref[4 * C:4 * C + 16, :] = wants[...].astype(BF)
+    got_ref[sp] = own_ref[...]
     pl.semaphore_wait(barrier, len(near_by))
 
     rows = [pl.ds(0, SPLIT), pl.ds(SPLIT, own_ref.shape[0] - SPLIT)]
@@ -276,7 +303,6 @@
         send(0, 0, 0, (way, 0))
     for dx in (1, -1, 2):
         send(1, 0, 0, (0, dx))
-    got_ref[sp] = own_ref[...]
 
     for k in range(4):
         for dx in (0, 1, -1, 2):
@@ -303,139 +329,139 @@
         one.wait_send()
 
 
-def gather_blocks(own):
+def gather_blocks(features, targets):
     vmem = pl.BlockSpec(memory_space=pltpu.VMEM)
+    rows = 4 * C + 16
     return pl.pallas_call(
         gather_kernel,
-        out_shape=jax.ShapeDtypeStruct((N_Z * N_X, *own.shape), own.dtype),
-        in_specs=[vmem],
+        out_shape=jax.ShapeDtypeStruct((N_Z * N_X, rows, 128), BF),
+        in_specs=[vmem, vmem],
         out_specs=vmem,
-        scratch_shapes=[pltpu.SemaphoreType.DMA((64,)), pltpu.SemaphoreType.DMA((2, N_Z * N_X))],
+        scratch_shapes=[
+            pltpu.VMEM((rows, 128), BF), pltpu.VMEM((16, 128), F32),
+            pltpu.SemaphoreType.DMA((64,)), pltpu.SemaphoreType.DMA((2, N_Z * N_X))],
         compiler_params=pltpu.CompilerParams(collective_id=1, has_side_effects=True),
-    )(own)
-
-
-def grad_sum_kernel(g_ref, out_ref, send_buf, rs_buf, dp_buf, ag_buf, send_sem, rs_sem, dp_send, dp_sem, ag_send, ag_sem):
+    )(features, targets)
+
+
+def grad_sum_kernel(g_ref, first_ref, second_ref, head_ref, pair_out, pair_in, send_buf, rs_buf, y_buf, done,
+                    pair_send, pair_sem, rs_send, rs_sem, y_send, y_sem, ag_send, ag_sem, last_send, last_sem):
     dp, sp = lax.axis_index("dp"), lax.axis_index("space")
-    n_dp, n_sp = dp_buf.shape[0], rs_buf.shape[0]
-    rows = rs_buf.shape[1]
+    core, y = lax.rem(dp, 2), lax.div(dp, 2)
+    n_y, n_sp = y_buf.shape[0], rs_buf.shape[0]
+    partner = (dp + 1 - 2 * core, sp)
+
+    def along(r):
+        return lax.rem(sp + r, n_sp)
+
+    def line(r):
+        return (lax.rem(y + r, n_y) * 2 + core, sp)
 
     barrier = pltpu.get_barrier_semaphore()
-
-    @pl.loop(1, n_sp)
-    def _(r):
-        pl.semaphore_signal(barrier, inc=1, device_id=(dp, lax.rem(sp + r, n_sp)), device_id_type=MESH)
-
-    @pl.loop(1, n_dp)
-    def _(r):
-        pl.semaphore_signal(barrier, inc=1, device_id=(lax.rem(dp + r, n_dp), sp), device_id_type=MESH)
-
-    send_buf[...] = g_ref[...].astype(jnp.bfloat16)
-    pl.semaphore_wait(barrier, n_sp + n_dp - 2)
+    pl.semaphore_signal(barrier, inc=1, device_id=partner, device_id_type=MESH)
+    for r in range(1, n_sp):
+        pl.semaphore_signal(barrier, inc=1, device_id=(dp, along(r)), device_id_type=MESH)
+    for r in range(1, n_y):
+        pl.semaphore_signal(barrier, inc=1, device_id=line(r), device_id_type=MESH)
+    pair_out[...] = g_ref[1 - core].astype(BF)
+    pl.semaphore_wait(barrier, n_sp + n_y - 1)
+
+    def remote(source, target, send, receive, device):
+        return pltpu.make_async_remote_copy(
+            src_ref=source, dst_ref=target, send_sem=send, recv_sem=receive, device_id=device, device_id_type=MESH)
+
+    pair_copy = remote(pair_out, pair_in, pair_send, pair_sem, partner)
+    pair_copy.start()
+    pair_copy.wait_recv()
+    send_buf[...] = (g_ref[core] + pair_in[...].astype(F32)).astype(BF)
 
     def rs_copy(r):
-        peer = lax.rem(sp + r, n_sp)
-        return pltpu.make_async_remote_copy(
-            src_ref=send_buf.at[peer], dst_ref=rs_buf.at[r], send_sem=send_sem.at[r], recv_sem=rs_sem.at[r],
-            device_id=(dp, peer), device_id_type=MESH)
-
-    def dp_copy(r):
-        peer = lax.rem(dp + r, n_dp)
-        return pltpu.make_async_remote_copy(
-            src_ref=dp_buf.at[0], dst_ref=dp_buf.at[r], send_sem=dp_send.at[r], recv_sem=dp_sem.at[r],
-            device_id=(peer, sp), device_id_type=MESH)
+        return remote(send_buf.at[along(r)], rs_buf.at[r], rs_send.at[r], rs_sem.at[r], (dp, along(r)))
+
+    def y_copy(r):
+        return remote(y_buf.at[0], y_buf.at[r], y_send.at[r], y_sem.at[r], line(r))
 
     def ag_copy(r):
-        peer = lax.rem(sp + r, n_sp)
-        return pltpu.make_async_remote_copy(
-            src_ref=ag_buf.at[0], dst_ref=ag_buf.at[r], send_sem=ag_send.at[r], recv_sem=ag_sem.at[r],
-            device_id=(dp, peer), device_id_type=MESH)
-
-    @pl.loop(1, n_sp)
-    def _(r):
+        return remote(done.at[core, sp], done.at[core, sp], ag_send.at[r], ag_sem.at[r], (dp, along(r)))
+
+    def last_copy(r):
+        slot = lax.rem(sp - r + n_sp, n_sp)
+        return remote(done.at[core, slot], done.at[core, slot], last_send.at[r], last_sem.at[r], partner)
+
+    for r in range(1, n_sp):
         rs_copy(r).start()
-
-    def add_rs(r, total):
+    total = g_ref[core, sp] + pair_in[sp].astype(F32)
+    for r in range(1, n_sp):
         rs_copy(r).wait_recv()
-        return total + rs_buf[r].astype(jnp.float32)
-
-    own = g_ref[sp]
-    total = lax.fori_loop(1, n_sp, add_rs, own)
-    dp_buf[0] = total.astype(jnp.bfloat16)
-
-    @pl.loop(1, n_dp)
-    def _(r):
-        dp_copy(r).start()
-
-    @pl.loop(1, n_dp)
-    def _(r):
-        dp_copy(r).wait_recv()
-
-    def add_dp(d, total):
-        return total + dp_buf[lax.rem(dp - d + n_dp, n_dp)].astype(jnp.float32)
-
-    total = lax.fori_loop(0, n_dp, add_dp, jnp.zeros((rows, 128), jnp.float32))
-    ag_buf[0] = total.astype(jnp.bfloat16)
-
-    @pl.loop(1, n_sp)
-    def _(r):
+        total = total + rs_buf[r].astype(F32)
+    y_buf[0] = total.astype(BF)
+    for r in range(1, n_y):
+        y_copy(r).start()
+    for r in range(1, n_y):
+        y_copy(r).wait_recv()
+    total = jnp.zeros(total.shape, F32)
+    for d in range(n_y):
+        total = total + y_buf[lax.rem(y - d + n_y, n_y)].astype(F32)
+    done[core, sp] = total.astype(BF)
+    for r in range(1, n_sp):
         ag_copy(r).start()
-
-    @pl.loop(1, n_sp)
-    def _(r):
+    last_copy(0).start()
+    for r in range(1, n_sp):
+        slot = lax.rem(sp - r + n_sp, n_sp)
+        remote(done.at[core, slot], done.at[core, slot], ag_send.at[r], ag_sem.at[r], (dp, along(r))).wait_recv()
+        last_copy(r).start()
+    for r in range(n_sp):
+        slot = lax.rem(sp - r + n_sp, n_sp)
+        remote(done.at[1 - core, slot], done.at[1 - core, slot], last_send.at[r], last_sem.at[r], partner).wait_recv()
+
+    for part, out in enumerate((first_ref, second_ref)):
+        for group in range(9):
+            a, rows = group // 3, slice(group % 3 * 16, group % 3 * 16 + 16)
+            tail = done[part, 27 + group // 2].astype(F32)
+            out[a * 9 + 8, rows, :] = tail[:, 64 * (group % 2):64 * (group % 2) + C]
+            wide = jnp.concatenate([done[part, group * 3 + col].astype(F32) for col in range(3)], axis=1)
+            for bc in range(8):
+                out[a * 9 + bc, rows, :] = wide[:, bc * C:(bc + 1) * C]
+    head_ref[...] = done[0, 31].astype(F32)[0:3, 64:64 + C]
+
+    pair_copy.wait_send()
+    for r in range(1, n_sp):
         rs_copy(r).wait_send()
-
-    @pl.loop(1, n_dp)
-    def _(r):
-        dp_copy(r).wait_send()
-
-    out_ref[sp] = ag_buf[0].astype(jnp.float32)
-
-    @pl.loop(1, n_sp)
-    def _(r):
-        ag_copy(r).wait_recv()
-        source = lax.rem(sp - r + n_sp, n_sp)
-        out_ref[source] = ag_buf[r].astype(jnp.float32)
-
-    @pl.loop(1, n_sp)
-    def _(r):
         ag_copy(r).wait_send()
-
-
-def grad_sum(flat):
-    n_dp, n_sp = lax.axis_size("dp"), lax.axis_size("space")
-    rows = flat.shape[1]
+    for r in range(1, n_y):
+        y_copy(r).wait_send()
+    for r in range(n_sp):
+        last_copy(r).wait_send()
+
+
+def grad_sum(grads):
+    n_y, n_sp = lax.axis_size("dp") // 2, lax.axis_size("space")
     vmem = pl.BlockSpec(memory_space=pltpu.VMEM)
     dma = pltpu.SemaphoreType.DMA
+    half = pltpu.VMEM((n_sp, 16, 128), BF)
+    kernel = jax.ShapeDtypeStruct((27, C, C), F32)
     return pl.pallas_call(
         grad_sum_kernel,
-        out_shape=jax.ShapeDtypeStruct(flat.shape, jnp.float32),
+        out_shape=(kernel, kernel, jax.ShapeDtypeStruct((3, C), F32)),
         in_specs=[vmem],
-        out_specs=vmem,
+        out_specs=(vmem, vmem, vmem),
         scratch_shapes=[
-            pltpu.VMEM((n_sp, rows, 128), jnp.bfloat16),
-            pltpu.VMEM((n_sp, rows, 128), jnp.bfloat16),
-            pltpu.VMEM((n_dp, rows, 128), jnp.bfloat16),
-            pltpu.VMEM((n_sp, rows, 128), jnp.bfloat16),
-            dma((n_sp,)), dma((n_sp,)), dma((n_dp,)), dma((n_dp,)), dma((n_sp,)), dma((n_sp,)),
+            half, half, half, half, pltpu.VMEM((n_y, 16, 128), BF), pltpu.VMEM((2, n_sp, 16, 128), BF),
+            dma, dma, dma((n_sp,)), dma((n_sp,)), dma((n_y,)), dma((n_y,)), dma((n_sp,)), dma((n_sp,)),
+            dma((n_sp,)), dma((n_sp,)),
         ],
         compiler_params=pltpu.CompilerParams(collective_id=0, has_side_effects=True),
-    )(flat)
+    )(grads)
 
 
 def on_device(features, device_block, conv_first, conv_second, head_weight, targets):
     n_dp, n_sp = lax.axis_size("dp"), lax.axis_size("space")
     scale = (n_dp * n_sp * 3 * 512) ** (-0.5)
-    got = gather_blocks(payload(features[0, 0], targets[0, 0]))
-    head = jnp.pad(head_weight, ((0, 13), (0, 0)))
+    got = gather_blocks(features, targets)
     logits, grads = compute_block(
-        device_block, got, stacked(conv_first), stacked(conv_second), stacked_back(conv_second), head, head.T, scale)
-    logits = logits[:, :3].reshape(8, 3, 16, 16)[:, :, 4:12, 4:12].transpose(1, 0, 2, 3).reshape(3, 512)
-    tiles = grads.reshape(6, C, 4, 128).transpose(0, 2, 1, 3).reshape(24, C, 128)
-    tiles = grad_sum(jnp.pad(tiles, ((0, n_sp - 24), (0, 0), (0, 0))))[:24]
-    grads = tiles.reshape(2, 3, 4, C, 128).transpose(0, 3, 1, 2, 4).reshape(2, C, 3, 512)
-    kernels = grads[..., :9 * C].reshape(2, C, 27, C)
-    return (logits[None, None], kernels[0], kernels[1], grads[0, :3, 0, 9 * C:10 * C])
+        device_block, got, conv_first.transpose(1, 0, 2), conv_second.transpose(1, 0, 2), head_weight, scale)
+    first, second, head = grad_sum(grads)
+    return (logits[None, None], first.transpose(1, 0, 2), second.transpose(1, 0, 2), head)
 
 
 def solution(mesh):

time: 113 us -> 92.4 us (0.82)
  local copies, waits for them, and re-layouts: 17.3 us -> 6.05 us
  Pallas kernels: 92.5 us -> 85.4 us
  other arithmetic: 1.39 us -> 0 us
    pallas_call x1, Pallas kernels: 42.4 us -> 34.9 us  [grad_sum(): pl.pallas_call(grad_sum_kernel, out_shape=(kernel, kernel, jax.ShapeDtype...]
    reshape x9 -> x0, local copies, waits for them, and re-layouts: 3.51 us -> none  [the longest x2 1.29 us: on_device(): grads.reshape(6, C, 4, 128).transpose(0, 2, 1, 3).reshape(24, C, 128)]
    slice x6 -> x0, local copies, waits for them, and re-layouts: 2.41 us -> none  [the longest x1 1.1 us: on_device(): tiles = grad_sum(jnp.pad(tiles, ((0, n_sp - 24), (0, 0), (0, 0))))[:24]]
    transpose x4 -> x0, local copies, waits for them, and re-layouts: 2.09 us -> none  [the longest x2 1.39 us: stacked(): return kernel.reshape(C, 3, 9 * C).transpose(1, 0, 2).reshape(3 * C, 9 * C)]
    squeeze x3 -> x0, local copies, waits for them, and re-layouts: 1.73 us -> none  [the longest x1 0.65 us: on_device(): grads[0, :3, 0, 9 * C:10 * C]]
    unnamed x8 -> x9, local copies, waits for them, and re-layouts: 4.5 us -> 6.05 us
    pad x3 -> x0, local copies, waits for them, and re-layouts: 1.54 us -> none  [the longest x1 0.94 us: on_device(): tiles = grad_sum(jnp.pad(tiles, ((0, n_sp - 24), (0, 0), (0, 0))))[:24]]
    another operation x3 -> x0, local copies, waits for them, and re-layouts: 1.53 us -> none  [the longest x2 0.83 us: payload(): feats = features.reshape(C, 4, 128).transpose(1, 0, 2).reshape(4 * C, 128)]
where the time goes in v3:
time: 92.4 us; the launch traced here: 92.1 us
  Pallas kernels  85.4 us (92%)
  local copies, waits for them, and re-layouts  6.05 us (7%)
    pallas_call x1, Pallas kernels, grad_sum(): pl.pallas_call(grad_sum_kernel, out_shape=(kernel, kernel, jax.ShapeDtype...  34.9 us
    pallas_call x1, Pallas kernels, gather_blocks(): pl.pallas_call(gather_kernel, out_shape=jax.ShapeDtypeStruct((N_Z * N_X,...  30.5 us
    pallas_call x1, Pallas kernels, compute_block(): pl.pallas_call(functools.partial(compute_kernel, scale), out_shape=(jax.S...  20 us
    unnamed x9, local copies, waits for them, and re-layouts  6.05 us

profile of v3, /device:TPU:1, one launch (start us, length us, event | category | flops | bytes accessed | tf_op | source)
XLA Modules:
  0.0 92.1 jit_solution(3105678677027188328)
XLA Ops:
  0.6 1.3 %copy.10.targets_ref = s32[1,1,3,512]{3,2,1,0:T(4,128)} copy(s32[1,1,3,512]{3,1,2,0:T(1,128)} %param.11) | data formatting | bytes 12288 | tf_op args[5]
  1.9 30.5 %shard_map.93.got_ref = bf16[32,208,128]{2,1,0:T(8,128)(2,1)} custom-call(bf16[1,1,48,512]{3,2,1,0:T(8,128)(2,1)} %features_ref.1, s32[1,1,3,512]{3,2,1,0:T(4,128)} %copy.10.targets_ref), custom_call_target="tpu_custom_call" | custom-call | tf_op jit(solution)/shard_map/pallas_call | solution.py:335
  32.4 20.0 %shard_map.94 = (f32[3,512]{1,0:T(4,128)}, f32[2,32,16,128]{3,2,1,0:T(8,128)}) custom-call(s32[1,32]{1,0:T(1,128)} %ids_ref.1, bf16[32,208,128]{2,1,0:T(8,128)(2,1)} %shard_map.93.got_ref, bf16[27,48,48]{2,1,0:T(8,128)(2,1)} %bitcast.7, bf16[27,48,48]{2,1,0:T(8,128)(2,1)} %bitcast.8, bf16[3,48]{1,0:T(4,128)(2,1)} %head_in_ref.1), custom_call_target="tpu_custom_call" | custom-call | tf_op jit(solution)/shard_map/pallas_call | solution.py:224
  52.4 1.3 %copy.11 = f32[1,1,3,512]{3,1,2,0:T(1,128)} copy(f32[1,1,3,512]{3,2,1,0:T(4,128)} %bitcast.9) | data formatting | bytes 12288
  53.7 34.9 %shard_map.95 = (f32[27,48,48]{2,1,0:T(8,128)}, f32[27,48,48]{2,1,0:T(8,128)}, f32[3,48]{1,0:T(4,128)}) custom-call(f32[2,32,16,128]{3,2,1,0:T(8,128)} %get-tuple-element.10.g_ref), custom_call_target="tpu_custom_call" | custom-call | tf_op jit(solution)/shard_map/pallas_call | solution.py:443
  88.6 0.0 copy-start
  88.6 0.0 copy-start.1
  88.6 2.0 %copy.15 = f32[48,27,48]{2,0,1:T(8,128)} copy(f32[48,27,48]{2,0,1:T(8,128)} %bitcast.6) | data formatting | bytes 497664
  90.6 0.0 copy-done
  90.6 0.8 copy.16
  91.5 0.0 copy-done.1
  91.5 0.6 copy.17
Async XLA Ops:
  88.6 2.1 %copy-start = (f32[27,48,48]{2,1,0:T(8,128)S(1)}, f32[27,48,48]{2,1,0:T(8,128)}, u32[]{:S(2)}) copy-start(f32[27,48,48]{2,1,0:T(8,128)} %get-tuple-element.12) | copy-start | bytes 746500
  88.6 2.9 %copy-start.1 = (f32[3,48]{1,0:T(4,128)S(1)}, f32[3,48]{1,0:T(4,128)}, u32[]{:S(2)}) copy-start(f32[3,48]{1,0:T(4,128)} %get-tuple-element.25) | copy-start | bytes 1732

commit v4 on v3

--- a/solution.py
+++ b/solution.py
@@ -39,8 +39,8 @@
 
 def compute_kernel(scale, ids_ref, got_ref, k1_ref, k2_ref, head_in_ref,
                    logits_ref, grads_ref,
-                   table, near, near_t, wide1, out1, pre1, wide2, out2, wide_b, out_b, lhs2, lhs1, want, mask_ref,
-                   head_acc, w1_ref, w2_ref, wb_ref, head_ref, raw_logits):
+                   table, near, near_t, faces, wide1, out1, pre1, wide2, out2, wide_b, out_b, lhs2, lhs1, want,
+                   mask_ref, mask2, hid2, slope2, back2, w1_ref, w2_ref, wb_ref, head_ref, raw_logits):
     me = lax.axis_index("space")
 
     for t in range(27):
@@ -74,62 +74,65 @@
 
     low_half = lax.broadcasted_iota(jnp.int32, (C, 128), 1) < 64
 
-    def tiles_of(bx, row, rows):
+    def tiles_of(bx, by, row, rows):
         return [
-            (got_ref[slots[bx * 9 + j], row:row + rows, :].astype(F32) * present[bx * 9 + j]).astype(BF)
-            for j in range(9)
+            (got_ref[slots[t], row:row + rows, :].astype(F32) * present[t]).astype(BF)
+            for t in (bx * 9 + by * 3 + bz for bz in range(3))
         ]
 
-    def face_tiles(tiles, half):
-        rows = tiles[0].shape[0]
-        keep = low_half[:rows]
+    def face_pair(tiles, half):
+        keep = low_half[:tiles[0].shape[0]]
         flip = lambda v: pltpu.roll(v, 64, 1)
-        for k in range(5):
-            low = tiles[2 * k] if half == 0 else flip(tiles[2 * k])
-            if k == 4:
-                high = jnp.zeros_like(low)
-            else:
-                high = tiles[2 * k + 1] if half == 1 else flip(tiles[2 * k + 1])
-            yield k, jnp.where(keep, low, high)
+        first = tiles[0] if half == 0 else flip(tiles[0])
+        second = tiles[1] if half == 1 else flip(tiles[1])
+        third = tiles[2] if half == 0 else flip(tiles[2])
+        return jnp.where(keep, first, second), jnp.where(keep, third, jnp.zeros_like(third))
 
     for bx in range(3):
+        for by in range(3):
+            for pair in range(4):
+                spots = [(half, bx * 8 + pair * 2 + half - 3) for half in range(2)]
+                spots = [(half, at) for half, at in spots if 0 <= at < 18]
+                if not spots:
+                    continue
+                tiles = tiles_of(bx, by, pair * C, C)
+                for half, at in spots:
+                    for k, value in enumerate(face_pair(tiles, half)):
+                        near[by, at * C:(at + 1) * C, k * 128:(k + 1) * 128] = value
+            tiles = tiles_of(bx, by, 4 * C, 16)
+            for half in range(2):
+                at = bx * 2 + half
+                for k, value in enumerate(face_pair(tiles, half)):
+                    near_t[by, at * 16:(at + 1) * 16, k * 128:(k + 1) * 128] = value
+
+    column = lax.broadcasted_iota(jnp.int32, (1, 3 * 128), 1)
+    z = (column & 15) + (column >> 7) + 3
+    source = (z >> 3) * 64 + ((column >> 4) & 7) * 8 + (z & 7)
+    pick_z = jnp.where(lax.broadcasted_iota(jnp.int32, (LANES, 3 * 128), 0) == source, 1.0, 0.0).astype(BF)
+    want[...] = jnp.zeros_like(want)
+    wanted = [dot32(near_t[by], pick_z[:, 128:256]) for by in range(3)]
+    for by in range(3):
+        faces[by] = dot32(near[by], pick_z).astype(BF)
+
+    def window(plane_24, start):
+        return pltpu.roll(plane_24, 384 - start, 1)[:, :LANES]
+
+    @pl.loop(0, 18)
+    def _(at):
+        rows = pl.ds(pl.multiple_of(at * C, 16), C)
+        for c in range(3):
+            tall = jnp.concatenate([faces[by, rows, c * 128:(c + 1) * 128] for by in range(3)], axis=1)
+            for b in range(3):
+                wide1[(b * 3 + c) * C:(b * 3 + c + 1) * C, plane(at)] = window(tall, 48 + 16 * b)
+
+    for at in range(6):
+        tall = window(jnp.concatenate([one[at * 16:(at + 1) * 16] for one in wanted], axis=1), 64)
         for pair in range(4):
-            spots = [(half, bx * 8 + pair * 2 + half - 3) for half in range(2)]
-            spots = [(half, at) for half, at in spots if 0 <= at < 18]
-            if not spots:
-                continue
-            tiles = tiles_of(bx, pair * C, C)
-            for half, at in spots:
-                for k, value in face_tiles(tiles, half):
-                    near[at * C:(at + 1) * C, k * 128:(k + 1) * 128] = value
-        tiles = tiles_of(bx, 4 * C, 16)
-        for half in range(2):
-            for k, value in face_tiles(tiles, half):
-                near_t[(bx * 2 + half) * 16:(bx * 2 + half + 1) * 16, k * 128:(k + 1) * 128] = value
+            xo = (at // 2 - 1) * 8 + pair * 2 + at % 2 + 4
+            if 2 <= xo < 14:
+                want[0:3, plane(xo - 2)] = tall[pair * 4:pair * 4 + 3]
 
     lane = lax.broadcasted_iota(jnp.int32, (1, LANES), 1)
-    face_row = lax.broadcasted_iota(jnp.int32, (640, LANES), 0)
-
-    def select_of(b, c):
-        y = (lane >> 4) + (b + 3)
-        z = (lane & 15) + (c + 3)
-        source = ((y >> 3) * 3 + (z >> 3)) * 64 + (y & 7) * 8 + (z & 7)
-        return jnp.where(face_row == source, 1.0, 0.0).astype(BF)
-
-    @pl.loop(0, 9)
-    def _(bc):
-        picked = dot32(near[...], select_of(bc // 3, bc % 3)).astype(BF)
-        rows = pl.ds(pl.multiple_of(bc * C, 16), C)
-        for at in range(18):
-            wide1[rows, plane(at)] = picked[at * C:(at + 1) * C]
-
-    picked_t = dot32(near_t[...], select_of(1, 1))
-    want[...] = jnp.zeros_like(want)
-    for xo in range(2, 14):
-        bx, x = (xo + 4) // 8, (xo + 4) % 8
-        row = (bx * 2 + x % 2) * 16 + (x // 2) * 4
-        want[xo - 2, 0:3, :] = picked_t[row:row + 3]
-
     y, z = lane >> 4, lane & 15
     region = ((y + 4) >> 3) * 3 + ((z + 4) >> 3)
     inner = jnp.where((y >= 2) & (y < 14) & (z >= 2) & (z < 14), 1.0, 0.0)
@@ -139,55 +142,63 @@
         for j in range(9):
             row = jnp.where(region == j, present[bx * 9 + j], row)
         mask_ref[bx, 0:1, :] = row
-        mask_ref[bx, 1:2, :] = row * inner
-
-    def region_of(xo):
-        return jnp.where(xo >= 12, 2, jnp.where(xo >= 4, 1, 0))
+        for xo in range(2, 14):
+            if (xo + 4) // 8 == bx:
+                mask2[0:1, plane(xo - 2)] = row * inner
+                mask2[1:2, plane(xo - 2)] = own_lane if bx == 1 else jnp.zeros_like(own_lane)
 
     out1[...] = dot32(w1_ref[...], wide1[...])
 
-    @pl.loop(0, 16)
-    def _(xo):
+    def first_plane(xo, carry):
         pre = out1[0:C, plane(xo)] + out1[C:2 * C, plane(xo + 1)] + out1[2 * C:3 * C, plane(xo + 2)]
         pre1[xo] = pre
         act, _slope = elu_pair(pre)
-        hid = (act * mask_ref[region_of(xo), 0:1, :]).astype(BF)
+        hid = (act * mask_ref[lax.div(xo + 4, 8), 0:1, :]).astype(BF)
         for bc in range(9):
             shift = -(32 * (bc // 3 - 1) + 2 * (bc % 3 - 1)) % LANES
             wide2[bc * C:(bc + 1) * C, plane(xo)] = pltpu.roll(hid, shift, 1) if shift else hid
+        return carry
+
+    lax.fori_loop(0, 16, first_plane, 0, unroll=2)
 
     out2[...] = dot32(w2_ref[...], wide2[...])
     lhs2[...] = jnp.zeros_like(lhs2)
     lhs1[...] = jnp.zeros_like(lhs1)
-    head_acc[...] = jnp.zeros_like(head_acc)
-
-    def second(xo, is_own):
-        pre = out2[0:C, plane(xo - 2)] + out2[C:2 * C, plane(xo)] + out2[2 * C:3 * C, plane(xo + 2)]
+
+    def second_plane(i, carry):
+        pre = out2[0:C, plane(i)] + out2[C:2 * C, plane(i + 2)] + out2[2 * C:3 * C, plane(i + 4)]
         act, slope = elu_pair(pre)
-        mask = mask_ref[region_of(xo), 1:2, :]
-        hid = (act * mask).astype(BF)
-        logits = dot32(head, hid)
-        grad_logit = ((jax.nn.sigmoid(logits) - want[xo - 2]) * mask * scale).astype(BF)
-        back = dot32(head_t, grad_logit)
-        grad_pre = (back * slope * mask).astype(BF)
+        mask = mask2[0:1, plane(i)]
+        hid2[:, plane(i)] = (act * mask).astype(BF)
+        slope2[:, plane(i)] = slope * mask
+        return carry
+
+    lax.fori_loop(0, 12, second_plane, 0, unroll=2)
+    logits = dot32(head, hid2[...])
+    for x in range(8):
+        raw_logits[x * 8:(x + 1) * 8, :] = logits[0:8, (x + 2) * LANES:(x + 3) * LANES]
+    grad_logit = (jax.nn.sigmoid(logits) - want[...]) * mask2[0:1, :] * scale
+    own_logit = (grad_logit * mask2[1:2, :]).astype(BF)
+    back2[...] = dot32(head_t, grad_logit.astype(BF))
+    head_grad = lax.dot_general(own_logit, hid2[...], NT, preferred_element_type=F32)
+
+    def grad_plane(i, is_own):
+        grad_pre = (back2[:, plane(i)] * slope2[:, plane(i)]).astype(BF)
         for bc in range(9):
             shift = (32 * (bc // 3 - 1) + 2 * (bc % 3 - 1)) % LANES
-            wide_b[bc * C:(bc + 1) * C, plane(xo - 2)] = pltpu.roll(grad_pre, shift, 1) if shift else grad_pre
+            wide_b[bc * C:(bc + 1) * C, plane(i)] = pltpu.roll(grad_pre, shift, 1) if shift else grad_pre
         if is_own:
-            raw_logits[pl.ds(pl.multiple_of((xo - 4) * 8, 8), 8), :] = logits[0:8]
-            own_logit = (grad_logit.astype(F32) * own_lane).astype(BF)
-            head_acc[...] += lax.dot_general(own_logit, hid, NT, preferred_element_type=F32)
             own_pre = (grad_pre.astype(F32) * own_lane).astype(BF)
             for a in range(3):
-                lhs2[a * C:(a + 1) * C, plane(xo + 2 * a - 4)] = own_pre
-
-    @pl.loop(0, 8)
-    def _(i):
-        second(i + 4, True)
-
-    @pl.loop(0, 4)
-    def _(i):
-        second(jnp.where(i < 2, i + 2, i + 10), False)
+                lhs2[a * C:(a + 1) * C, plane(i + 2 * a - 2)] = own_pre
+
+    def own_plane(i, carry):
+        grad_plane(i + 2, True)
+        return carry
+
+    lax.fori_loop(0, 8, own_plane, 0, unroll=2)
+    for i in (0, 1, 10, 11):
+        grad_plane(i, False)
 
     grads_ref[:, 27:32] = jnp.zeros((2, 5, 16, 128), F32)
     pack_grads(grads_ref, 1, lax.dot_general(
@@ -203,7 +214,7 @@
             lhs1[a * C:(a + 1) * C, plane(q + a - 4)] = grad_pre
 
     pack_grads(grads_ref, 0, lax.dot_general(
-        lhs1[...], wide1[:, 4 * LANES:14 * LANES], NT, preferred_element_type=F32), head_acc[...])
+        lhs1[...], wide1[:, 4 * LANES:14 * LANES], NT, preferred_element_type=F32), head_grad)
 
     high = raw_logits[...].astype(BF)
     rest = raw_logits[...] - high.astype(F32)
@@ -228,12 +239,13 @@
         out_specs=(vmem, vmem),
         scratch_shapes=[
             pltpu.SMEM((64,), jnp.int32),
-            v((18 * C, 640), BF), v((96, 640), BF),
+            v((3, 18 * C, LANES), BF), v((3, 96, LANES), BF), v((3, 18 * C, 3 * 128), BF),
             v((9 * C, 18 * LANES), BF), v((3 * C, 18 * LANES), F32), v((16, C, LANES), F32),
             v((9 * C, 16 * LANES), BF), v((3 * C, 16 * LANES), F32),
             v((9 * C, 12 * LANES), BF), v((3 * C, 12 * LANES), F32),
             v((3 * C, 12 * LANES), BF), v((3 * C, 10 * LANES), BF),
-            v((12, 16, LANES), F32), v((3, 8, LANES), F32), v((16, C), F32),
+            v((16, 12 * LANES), F32), v((3, 8, LANES), F32), v((8, 12 * LANES), F32),
+            v((C, 12 * LANES), BF), v((C, 12 * LANES), F32), v((C, 12 * LANES), F32),
             v((3 * C, 9 * C), BF), v((3 * C, 9 * C), BF), v((9 * C, 3 * C), BF), v((16, C), F32),
             v((64, LANES), F32),
         ],
@@ -243,7 +255,9 @@
 
 MESH = pl.DeviceIdType.MESH
 N_Z, N_X = 8, 4
-SPLIT = 96
+SPLIT = 48
+Z_STEPS = (1, -1, 2, -2, 3, -3, 4)
+X_STEPS = (1, -1, 2)
 
 
 def gather_kernel(features_ref, targets_ref, got_ref, own_ref, wants, send_sem, recv_sem):
@@ -253,7 +267,7 @@
     def at(dz, dx):
         return lax.rem(z + dz + N_Z, N_Z) * N_X + lax.rem(x + dx + N_X, N_X)
 
-    near_by = [(1, 0), (-1, 0), (0, 1), (0, -1), (0, 2)]
+    near_by = [(dz, 0) for dz in Z_STEPS] + [(0, dx) for dx in X_STEPS]
     barrier = pltpu.get_barrier_semaphore()
     for dz, dx in near_by:
         pl.semaphore_signal(barrier, inc=1, device_id=(dp, at(dz, dx)), device_id_type=MESH)
@@ -282,49 +296,43 @@
         one.start()
         sent.append(one)
 
-    arrived = set()
-
     def await_block(half, dz, dx):
-        if (half, dz, dx) not in arrived and (dz, dx) != (0, 0):
-            slot = at(dz, dx)
-            pltpu.make_async_remote_copy(
-                src_ref=own_ref.at[rows[half]], dst_ref=got_ref.at[slot, rows[half]], send_sem=send_sem.at[0],
-                recv_sem=recv_sem.at[half, slot], device_id=(dp, at(0, 1)), device_id_type=MESH).wait_recv()
-            arrived.add((half, dz, dx))
-
-    def reach(way, dx):
-        return 4 if (way == 1) == (dx in (0, 1)) else 3
-
-    for way in (1, -1):
-        send(1, 0, 0, (way, 0))
-    for dx in (1, -1, 2):
+        slot = at(dz, dx)
+        pltpu.make_async_remote_copy(
+            src_ref=own_ref.at[rows[half]], dst_ref=got_ref.at[slot, rows[half]], send_sem=send_sem.at[0],
+            recv_sem=recv_sem.at[half, slot], device_id=(dp, at(0, 1)), device_id_type=MESH).wait_recv()
+
+    for dx in X_STEPS:
         send(0, 0, 0, (0, dx))
-    for way in (1, -1):
-        send(0, 0, 0, (way, 0))
-    for dx in (1, -1, 2):
+    for dz in Z_STEPS:
+        send(1, 0, 0, (dz, 0))
+    for dx in X_STEPS:
         send(1, 0, 0, (0, dx))
-
-    for k in range(4):
-        for dx in (0, 1, -1, 2):
-            for way in (1, -1):
-                if (k, dx) != (0, 0) and k < reach(way, dx):
-                    await_block(0, -way * k, dx)
-                    send(0, -way * k, dx, (way, 0))
-        for way in (1, -1):
-            far = k + 1
-            if far <= reach(way, 0):
-                await_block(1, -way * far, 0)
-                if far < reach(way, 0):
-                    send(1, -way * far, 0, (way, 0))
-                for dx in (1, -1, 2):
-                    send(1, -way * far, 0, (0, dx))
-
-    for half in range(2):
-        for dx in (0, 1, -1, 2):
-            column = dx if half == 0 else 0
-            for way in (1, -1):
-                for k in range(reach(way, column) + 1):
-                    await_block(half, -way * k, dx)
+    for dz in Z_STEPS:
+        send(0, 0, 0, (dz, 0))
+
+    def pass_x(dx):
+        await_block(0, 0, dx)
+        for dz in Z_STEPS:
+            send(0, 0, dx, (dz, 0))
+
+    def pass_z(dz):
+        await_block(1, dz, 0)
+        for dx in X_STEPS:
+            send(1, dz, 0, (0, dx))
+
+    for dz in (1, -1):
+        pass_z(dz)
+    for dx in X_STEPS:
+        pass_x(dx)
+    for dz in (2, -2, 3, -3, 4):
+        pass_z(dz)
+    for dz in Z_STEPS:
+        for dx in (0, *X_STEPS):
+            await_block(0, dz, dx)
+    for dz in (0, *Z_STEPS):
+        for dx in X_STEPS:
+            await_block(1, dz, dx)
     for one in sent:
         one.wait_send()
 

time: 92.4 us -> 89 us (0.963)
  Pallas kernels: 85.4 us -> 81.9 us
    pallas_call x1, Pallas kernels: 20 us -> 14.7 us  [compute_block(): pl.pallas_call(functools.partial(compute_kernel, scale), out_shape=(jax.S...]
    pallas_call x1, Pallas kernels: 30.5 us -> 32.2 us  [gather_blocks(): pl.pallas_call(gather_kernel, out_shape=jax.ShapeDtypeStruct((N_Z * N_X,...]
where the time goes in v4:
time: 89 us; the launch traced here: 88.6 us
  Pallas kernels  81.9 us (92%)
  local copies, waits for them, and re-layouts  6.05 us (7%)
    pallas_call x1, Pallas kernels, grad_sum(): pl.pallas_call(grad_sum_kernel, out_shape=(kernel, kernel, jax.ShapeDtype...  35 us
    pallas_call x1, Pallas kernels, gather_blocks(): pl.pallas_call(gather_kernel, out_shape=jax.ShapeDtypeStruct((N_Z * N_X,...  32.2 us
    pallas_call x1, Pallas kernels, compute_block(): pl.pallas_call(functools.partial(compute_kernel, scale), out_shape=(jax.S...  14.7 us
    unnamed x9, local copies, waits for them, and re-layouts  6.05 us

profile of v4, /device:TPU:1, one launch (start us, length us, event | category | flops | bytes accessed | tf_op | source)
XLA Modules:
  0.0 88.6 jit_solution(1795584480827860653)
XLA Ops:
  0.6 1.3 %copy.10.targets_ref = s32[1,1,3,512]{3,2,1,0:T(4,128)} copy(s32[1,1,3,512]{3,1,2,0:T(1,128)} %param.11) | data formatting | bytes 12288 | tf_op args[5]
  1.9 32.2 %shard_map.93.got_ref = bf16[32,208,128]{2,1,0:T(8,128)(2,1)} custom-call(bf16[1,1,48,512]{3,2,1,0:T(8,128)(2,1)} %features_ref.1, s32[1,1,3,512]{3,2,1,0:T(4,128)} %copy.10.targets_ref), custom_call_target="tpu_custom_call" | custom-call | tf_op jit(solution)/shard_map/pallas_call | solution.py:343
  34.1 14.7 %shard_map.94 = (f32[3,512]{1,0:T(4,128)}, f32[2,32,16,128]{3,2,1,0:T(8,128)}) custom-call(s32[1,32]{1,0:T(1,128)} %ids_ref.1, bf16[32,208,128]{2,1,0:T(8,128)(2,1)} %shard_map.93.got_ref, bf16[27,48,48]{2,1,0:T(8,128)(2,1)} %bitcast.7, bf16[27,48,48]{2,1,0:T(8,128)(2,1)} %bitcast.8, bf16[3,48]{1,0:T(4,128)(2,1)} %head_in_ref.1), custom_call_target="tpu_custom_call" | custom-call | tf_op jit(solution)/shard_map/pallas_call | solution.py:235
  48.8 1.3 %copy.11 = f32[1,1,3,512]{3,1,2,0:T(1,128)} copy(f32[1,1,3,512]{3,2,1,0:T(4,128)} %bitcast.9) | data formatting | bytes 12288
  50.1 35.0 %shard_map.95 = (f32[27,48,48]{2,1,0:T(8,128)}, f32[27,48,48]{2,1,0:T(8,128)}, f32[3,48]{1,0:T(4,128)}) custom-call(f32[2,32,16,128]{3,2,1,0:T(8,128)} %get-tuple-element.10.g_ref), custom_call_target="tpu_custom_call" | custom-call | tf_op jit(solution)/shard_map/pallas_call | solution.py:451
  85.1 0.0 copy-start
  85.1 0.0 copy-start.1
  85.1 2.0 %copy.15 = f32[48,27,48]{2,0,1:T(8,128)} copy(f32[48,27,48]{2,0,1:T(8,128)} %bitcast.6) | data formatting | bytes 497664
  87.2 0.0 copy-done
  87.2 0.8 copy.16
  88.0 0.0 copy-done.1
  88.0 0.6 copy.17
Async XLA Ops:
  85.1 2.1 %copy-start = (f32[27,48,48]{2,1,0:T(8,128)S(1)}, f32[27,48,48]{2,1,0:T(8,128)}, u32[]{:S(2)}) copy-start(f32[27,48,48]{2,1,0:T(8,128)} %get-tuple-element.12) | copy-start | bytes 746500
  85.1 2.9 %copy-start.1 = (f32[3,48]{1,0:T(4,128)S(1)}, f32[3,48]{1,0:T(4,128)}, u32[]{:S(2)}) copy-start(f32[3,48]{1,0:T(4,128)} %get-tuple-element.25) | copy-start | bytes 1732

commit v5 on v4

v5 whole, which is shorter than its diff:
```python
import functools
from types import SimpleNamespace

import jax
import jax.numpy as jnp
from jax import lax
from jax.experimental import pallas as pl
from jax.experimental.pallas import tpu as pltpu
from jax.sharding import PartitionSpec as P

BF = jnp.bfloat16
F32 = jnp.float32
C = 48
LANES = 256
NT = (((1,), (1,)), ((), ()))
TN = (((0,), (0,)), ((), ()))


def dot32(a, b):
    return jnp.dot(a, b, preferred_element_type=F32)


def elu_pair(values):
    negative = jnp.exp(jnp.minimum(values, 0.0))
    return (jnp.where(values > 0, values, negative - 1.0), jnp.where(values > 0, 1.0, negative))


def plane(index):
    start = index * LANES
    return pl.ds(start if isinstance(index, int) else pl.multiple_of(start, LANES), LANES)


def pack_grads(grads_ref, part, grads, head):
    for group in range(9):
        rows = grads[group * 16:(group + 1) * 16]
        for col in range(3):
            grads_ref[part, group * 3 + col] = rows[:, col * 128:(col + 1) * 128]
        grads_ref[part, 27 + group // 2, :, 64 * (group % 2):64 * (group % 2) + C] = rows[:, 384:9 * C]
    grads_ref[part, 31, :, 64:64 + C] = head


MESH = pl.DeviceIdType.MESH
N_Z, N_X, N_Y = 8, 4, 8
SPLIT = 48
Z_STEPS = (1, -1, 2, -2, 3, -3, 4)
X_STEPS = (1, -1, 2)


def gather_stage(features_ref, targets_ref, got_ref, own_ref, wants, send_sem, recv_sem, meanwhile):
    dp, sp = lax.axis_index("dp"), lax.axis_index("space")
    z, x = lax.div(sp, N_X), lax.rem(sp, N_X)

    def at(dz, dx):
        return lax.rem(z + dz + N_Z, N_Z) * N_X + lax.rem(x + dx + N_X, N_X)

    near_by = [(dz, 0) for dz in Z_STEPS] + [(0, dx) for dx in X_STEPS]
    barrier = pltpu.get_barrier_semaphore()
    for dz, dx in near_by:
        pl.semaphore_signal(barrier, inc=1, device_id=(dp, at(dz, dx)), device_id_type=MESH)
    others = [(dp + 1 - 2 * lax.rem(dp, 2), sp)] + [(lax.rem(dp + 2 * r, N_Y * 2), sp) for r in range(1, N_Y)]
    for other in others:
        pl.semaphore_signal(barrier, inc=1, device_id=other, device_id_type=MESH)

    wants[...] = jnp.zeros_like(wants)
    for pair in range(4):
        lanes = slice(pair * 128, (pair + 1) * 128)
        own_ref[pair * C:(pair + 1) * C, :] = features_ref[0, 0, :, lanes]
        wants[pair * 4:pair * 4 + 3, :] = targets_ref[0, 0, :, lanes].astype(F32)
    own_ref[4 * C:4 * C + 16, :] = wants[...].astype(BF)
    got_ref[sp] = own_ref[...]
    pl.semaphore_wait(barrier, len(near_by) + len(others))

    rows = [pl.ds(0, SPLIT), pl.ds(SPLIT, own_ref.shape[0] - SPLIT)]
    sent = []

    def copy(half, dz, dx, to, number):
        slot = at(dz, dx)
        source = own_ref.at[rows[half]] if (dz, dx) == (0, 0) else got_ref.at[slot, rows[half]]
        return pltpu.make_async_remote_copy(
            src_ref=source, dst_ref=got_ref.at[slot, rows[half]], send_sem=send_sem.at[number],
            recv_sem=recv_sem.at[half, slot], device_id=(dp, at(*to)), device_id_type=MESH)

    def send(half, dz, dx, to):
        one = copy(half, dz, dx, to, len(sent))
        one.start()
        sent.append(one)

    def await_block(half, dz, dx):
        slot = at(dz, dx)
        pltpu.make_async_remote_copy(
            src_ref=own_ref.at[rows[half]], dst_ref=got_ref.at[slot, rows[half]], send_sem=send_sem.at[0],
            recv_sem=recv_sem.at[half, slot], device_id=(dp, at(0, 1)), device_id_type=MESH).wait_recv()

    for dx in X_STEPS:
        send(0, 0, 0, (0, dx))
    for dz in Z_STEPS:
        send(1, 0, 0, (dz, 0))
    for dx in X_STEPS:
        send(1, 0, 0, (0, dx))
    for dz in Z_STEPS:
        send(0, 0, 0, (dz, 0))
    meanwhile()

    def pass_x(dx):
        await_block(0, 0, dx)
        for dz in Z_STEPS:
            send(0, 0, dx, (dz, 0))

    def pass_z(dz):
        await_block(1, dz, 0)
        for dx in X_STEPS:
            send(1, dz, 0, (0, dx))

    for dz in (1, -1):
        pass_z(dz)
    for dx in X_STEPS:
        pass_x(dx)
    for dz in (2, -2, 3, -3, 4):
        pass_z(dz)
    for dz in Z_STEPS:
        for dx in (0, *X_STEPS):
            await_block(0, dz, dx)
    for dz in (0, *Z_STEPS):
        for dx in X_STEPS:
            await_block(1, dz, dx)
    return sent


def prepare(s, ids_ref, k1_ref, k2_ref, head_in_ref):
    for t in range(27):
        a, bc = t // 9, t % 9
        s.w1_ref[a * C:(a + 1) * C, bc * C:(bc + 1) * C] = k1_ref[t]
        s.w2_ref[a * C:(a + 1) * C, bc * C:(bc + 1) * C] = k2_ref[t]
        s.wb_ref[bc * C:(bc + 1) * C, a * C:(a + 1) * C] = k2_ref[t]
    s.head_ref[...] = jnp.zeros_like(s.head_ref)
    s.head_ref[0:3, :] = head_in_ref[...].astype(F32)

    column = lax.broadcasted_iota(jnp.int32, (1, 3 * 128), 1)
    z = (column & 15) + (column >> 7) + 3
    source = (z >> 3) * 64 + ((column >> 4) & 7) * 8 + (z & 7)
    s.pick_ref[...] = jnp.where(lax.broadcasted_iota(jnp.int32, (LANES, 3 * 128), 0) == source, 1.0, 0.0).astype(BF)
    for ref in (s.want, s.lhs2, s.lhs1):
        ref[...] = jnp.zeros_like(ref)
    s.grads_ref[:, 27:32] = jnp.zeros((2, 5, 16, 128), F32)

    own = ids_ref[0, lax.axis_index("space")]
    ox, oy, oz = own // 16, own // 4 % 4, own % 4

    @pl.loop(0, 27)
    def _(t):
        x, y, z = ox + t // 9 - 1, oy + t // 3 % 3 - 1, oz + t % 3 - 1
        inside = (x >= 0) & (x < 4) & (y >= 0) & (y < 4) & (z >= 0) & (z < 4)
        wanted = jnp.where(inside, (x * 4 + y) * 4 + z, -1)
        found = jnp.int32(-1)
        for j in range(32):
            found = jnp.where(ids_ref[0, j] == wanted, j, found)
        s.table[t] = found


def compute(s, scale):
    slots = [jnp.maximum(s.table[t], 0) for t in range(27)]
    present = [jnp.where(s.table[t] >= 0, 1.0, 0.0).astype(F32) for t in range(27)]
    head = s.head_ref[...].astype(BF)
    head_t = s.head_ref[...].T.astype(BF)

    low_half = lax.broadcasted_iota(jnp.int32, (C, 128), 1) < 64

    def tiles_of(bx, by, row, rows):
        return [
            (s.got[slots[t], row:row + rows, :].astype(F32) * present[t]).astype(BF)
            for t in (bx * 9 + by * 3 + bz for bz in range(3))
        ]

    def face_pair(tiles, half):
        keep = low_half[:tiles[0].shape[0]]
        flip = lambda v: pltpu.roll(v, 64, 1)
        first = tiles[0] if half == 0 else flip(tiles[0])
        second = tiles[1] if half == 1 else flip(tiles[1])
        third = tiles[2] if half == 0 else flip(tiles[2])
        return jnp.where(keep, first, second), jnp.where(keep, third, jnp.zeros_like(third))

    for bx in range(3):
        for by in range(3):
            for pair in range(4):
                spots = [(half, bx * 8 + pair * 2 + half - 3) for half in range(2)]
                spots = [(half, at) for half, at in spots if 0 <= at < 18]
                if not spots:
                    continue
                tiles = tiles_of(bx, by, pair * C, C)
                for half, at in spots:
                    for k, value in enumerate(face_pair(tiles, half)):
                        s.near[by, at * C:(at + 1) * C, k * 128:(k + 1) * 128] = value
            tiles = tiles_of(bx, by, 4 * C, 16)
            for half in range(2):
                at = bx * 2 + half
                for k, value in enumerate(face_pair(tiles, half)):
                    s.near_t[by, at * 16:(at + 1) * 16, k * 128:(k + 1) * 128] = value

    wanted = [dot32(s.near_t[by], s.pick_ref[:, 128:256]) for by in range(3)]
    for by in range(3):
        s.faces[by] = dot32(s.near[by], s.pick_ref[...]).astype(BF)

    def window(plane_24, start):
        return pltpu.roll(plane_24, 384 - start, 1)[:, :LANES]

    @pl.loop(0, 18)
    def _(at):
        rows = pl.ds(pl.multiple_of(at * C, 16), C)
        for c in range(3):
            tall = jnp.concatenate([s.faces[by, rows, c * 128:(c + 1) * 128] for by in range(3)], axis=1)
            for b in range(3):
                s.wide1[(b * 3 + c) * C:(b * 3 + c + 1) * C, plane(at)] = window(tall, 48 + 16 * b)

    for at in range(6):
        tall = window(jnp.concatenate([one[at * 16:(at + 1) * 16] for one in wanted], axis=1), 64)
        for pair in range(4):
            xo = (at // 2 - 1) * 8 + pair * 2 + at % 2 + 4
            if 2 <= xo < 14:
                s.want[0:3, plane(xo - 2)] = tall[pair * 4:pair * 4 + 3]

    lane = lax.broadcasted_iota(jnp.int32, (1, LANES), 1)
    y, z = lane >> 4, lane & 15
    region = ((y + 4) >> 3) * 3 + ((z + 4) >> 3)
    inner = jnp.where((y >= 2) & (y < 14) & (z >= 2) & (z < 14), 1.0, 0.0)
    own_lane = jnp.where((y >= 4) & (y < 12) & (z >= 4) & (z < 12), 1.0, 0.0)
    for bx in range(3):
        row = jnp.zeros((1, LANES), F32)
        for j in range(9):
            row = jnp.where(region == j, present[bx * 9 + j], row)
        s.mask_ref[bx, 0:1, :] = row
        for xo in range(2, 14):
            if (xo + 4) // 8 == bx:
                s.mask2[0:1, plane(xo - 2)] = row * inner
                s.mask2[1:2, plane(xo - 2)] = own_lane if bx == 1 else jnp.zeros_like(own_lane)

    s.out1[...] = dot32(s.w1_ref[...], s.wide1[...])

    def first_plane(xo, carry):
        pre = s.out1[0:C, plane(xo)] + s.out1[C:2 * C, plane(xo + 1)] + s.out1[2 * C:3 * C, plane(xo + 2)]
        s.pre1[xo] = pre
        act, _slope = elu_pair(pre)
        hid = (act * s.mask_ref[lax.div(xo + 4, 8), 0:1, :]).astype(BF)
        for bc in range(9):
            shift = -(32 * (bc // 3 - 1) + 2 * (bc % 3 - 1)) % LANES
            s.wide2[bc * C:(bc + 1) * C, plane(xo)] = pltpu.roll(hid, shift, 1) if shift else hid
        return carry

    lax.fori_loop(0, 16, first_plane, 0, unroll=2)

    s.out2[...] = dot32(s.w2_ref[...], s.wide2[...])

    def second_plane(i, carry):
        pre = s.out2[0:C, plane(i)] + s.out2[C:2 * C, plane(i + 2)] + s.out2[2 * C:3 * C, plane(i + 4)]
        act, slope = elu_pair(pre)
        mask = s.mask2[0:1, plane(i)]
        s.hid2[:, plane(i)] = (act * mask).astype(BF)
        s.slope2[:, plane(i)] = slope * mask
        return carry

    lax.fori_loop(0, 12, second_plane, 0, unroll=2)
    logits = dot32(head, s.hid2[...])
    for x in range(8):
        s.raw_logits[x * 8:(x + 1) * 8, :] = logits[0:8, (x + 2) * LANES:(x + 3) * LANES]
    grad_logit = (jax.nn.sigmoid(logits) - s.want[...]) * s.mask2[0:1, :] * scale
    own_logit = (grad_logit * s.mask2[1:2, :]).astype(BF)
    s.back2[...] = dot32(head_t, grad_logit.astype(BF))
    head_grad = lax.dot_general(own_logit, s.hid2[...], NT, preferred_element_type=F32)

    def grad_plane(i, is_own):
        grad_pre = (s.back2[:, plane(i)] * s.slope2[:, plane(i)]).astype(BF)
        for bc in range(9):
            shift = (32 * (bc // 3 - 1) + 2 * (bc % 3 - 1)) % LANES
            s.wide_b[bc * C:(bc + 1) * C, plane(i)] = pltpu.roll(grad_pre, shift, 1) if shift else grad_pre
        if is_own:
            own_pre = (grad_pre.astype(F32) * own_lane).astype(BF)
            for a in range(3):
                s.lhs2[a * C:(a + 1) * C, plane(i + 2 * a - 2)] = own_pre

    def own_plane(i, carry):
        grad_plane(i + 2, True)
        return carry

    lax.fori_loop(0, 8, own_plane, 0, unroll=2)
    for i in (0, 1, 10, 11):
        grad_plane(i, False)

    pack_grads(s.grads_ref, 1, lax.dot_general(
        s.lhs2[...], s.wide2[:, 2 * LANES:14 * LANES], NT, preferred_element_type=F32), jnp.zeros((16, C), F32))
    s.out_b[...] = lax.dot_general(s.wb_ref[...], s.wide_b[...], TN, preferred_element_type=F32)

    @pl.loop(4, 12)
    def _(q):
        back = s.out_b[0:C, plane(q)] + s.out_b[C:2 * C, plane(q - 2)] + s.out_b[2 * C:3 * C, plane(q - 4)]
        _act, slope = elu_pair(s.pre1[q])
        grad_pre = (back * slope * own_lane).astype(BF)
        for a in range(3):
            s.lhs1[a * C:(a + 1) * C, plane(q + a - 4)] = grad_pre

    pack_grads(s.grads_ref, 0, lax.dot_general(
        s.lhs1[...], s.wide1[:, 4 * LANES:14 * LANES], NT, preferred_element_type=F32), head_grad)


def finish_logits(s, logits_ref):
    high = s.raw_logits[...].astype(BF)
    rest = s.raw_logits[...] - high.astype(F32)
    middle = rest.astype(BF)
    low = (rest - middle.astype(F32)).astype(BF)
    cell = lax.broadcasted_iota(jnp.int32, (1, 64), 1)
    source = ((cell >> 3) + 4) * 16 + (cell & 7) + 4
    pick = jnp.where(lax.broadcasted_iota(jnp.int32, (LANES, 64), 0) == source, 1.0, 0.0).astype(BF)
    parts = dot32(jnp.concatenate([high, middle, low], axis=0), pick)
    own_logits = (parts[0:64] + parts[64:128]) + parts[128:192]
    for x in range(8):
        logits_ref[:, x * 64:(x + 1) * 64] = own_logits[x * 8:x * 8 + 3]


def grad_sum_stage(s, g_ref, first_ref, second_ref, head_ref, meanwhile):
    pair_out, pair_in, send_buf, rs_buf, y_buf, done = (
        s.pair_out, s.pair_in, s.send_buf, s.rs_buf, s.y_buf, s.done)
    pair_send, pair_sem, rs_send, rs_sem = s.pair_send, s.pair_sem, s.rs_send, s.rs_sem
    y_send, y_sem, ag_send, ag_sem, last_send, last_sem = (
        s.y_send, s.y_sem, s.ag_send, s.ag_sem, s.last_send, s.last_sem)
    dp, sp = lax.axis_index("dp"), lax.axis_index("space")
    core, y = lax.rem(dp, 2), lax.div(dp, 2)
    n_y, n_sp = y_buf.shape[0], rs_buf.shape[0]
    partner = (dp + 1 - 2 * core, sp)

    def along(r):
        return lax.rem(sp + r, n_sp)

    def line(r):
        return (lax.rem(y + r, n_y) * 2 + core, sp)

    pair_out[...] = g_ref[1 - core].astype(BF)

    def remote(source, target, send, receive, device):
        return pltpu.make_async_remote_copy(
            src_ref=source, dst_ref=target, send_sem=send, recv_sem=receive, device_id=device, device_id_type=MESH)

    pair_copy = remote(pair_out, pair_in, pair_send, pair_sem, partner)
    pair_copy.start()
    pair_copy.wait_recv()
    send_buf[...] = (g_ref[core] + pair_in[...].astype(F32)).astype(BF)

    def rs_copy(r):
        return remote(send_buf.at[along(r)], rs_buf.at[r], rs_send.at[r], rs_sem.at[r], (dp, along(r)))

    def y_copy(r):
        return remote(y_buf.at[0], y_buf.at[r], y_send.at[r], y_sem.at[r], line(r))

    def ag_copy(r):
        return remote(done.at[core, sp], done.at[core, sp], ag_send.at[r], ag_sem.at[r], (dp, along(r)))

    def last_copy(r):
        slot = lax.rem(sp - r + n_sp, n_sp)
        return remote(done.at[core, slot], done.at[core, slot], last_send.at[r], last_sem.at[r], partner)

    for r in range(1, n_sp):
        rs_copy(r).start()
    meanwhile()
    total = g_ref[core, sp] + pair_in[sp].astype(F32)
    for r in range(1, n_sp):
        rs_copy(r).wait_recv()
        total = total + rs_buf[r].astype(F32)
    y_buf[0] = total.astype(BF)
    for r in range(1, n_y):
        y_copy(r).start()
    for r in range(1, n_y):
        y_copy(r).wait_recv()
    total = jnp.zeros(total.shape, F32)
    for d in range(n_y):
        total = total + y_buf[lax.rem(y - d + n_y, n_y)].astype(F32)
    done[core, sp] = total.astype(BF)
    for r in range(1, n_sp):
        ag_copy(r).start()
    last_copy(0).start()
    for r in range(1, n_sp):
        slot = lax.rem(sp - r + n_sp, n_sp)
        remote(done.at[core, slot], done.at[core, slot], ag_send.at[r], ag_sem.at[r], (dp, along(r))).wait_recv()
        last_copy(r).start()
    for r in range(n_sp):
        slot = lax.rem(sp - r + n_sp, n_sp)
        remote(done.at[1 - core, slot], done.at[1 - core, slot], last_send.at[r], last_sem.at[r], partner).wait_recv()

    for part, out in enumerate((first_ref, second_ref)):
        for group in range(9):
            a, rows = group // 3, slice(group % 3 * 16, group % 3 * 16 + 16)
            tail = done[part, 27 + group // 2].astype(F32)
            out[a * 9 + 8, rows, :] = tail[:, 64 * (group % 2):64 * (group % 2) + C]
            wide = jnp.concatenate([done[part, group * 3 + col].astype(F32) for col in range(3)], axis=1)
            for bc in range(8):
                out[a * 9 + bc, rows, :] = wide[:, bc * C:(bc + 1) * C]
    head_ref[...] = done[0, 31].astype(F32)[0:3, 64:64 + C]

    pair_copy.wait_send()
    for r in range(1, n_sp):
        rs_copy(r).wait_send()
        ag_copy(r).wait_send()
    for r in range(1, n_y):
        y_copy(r).wait_send()
    for r in range(n_sp):
        last_copy(r).wait_send()


SCRATCH = dict(
    table=pltpu.SMEM((32,), jnp.int32),
    got=pltpu.VMEM((32, 4 * C + 16, 128), BF), own=pltpu.VMEM((4 * C + 16, 128), BF), wants=pltpu.VMEM((16, 128), F32),
    near=pltpu.VMEM((3, 18 * C, LANES), BF), near_t=pltpu.VMEM((3, 96, LANES), BF),
    faces=pltpu.VMEM((3, 18 * C, 3 * 128), BF), pick_ref=pltpu.VMEM((LANES, 3 * 128), BF),
    wide1=pltpu.VMEM((9 * C, 18 * LANES), BF), out1=pltpu.VMEM((3 * C, 18 * LANES), F32),
    pre1=pltpu.VMEM((16, C, LANES), F32),
    wide2=pltpu.VMEM((9 * C, 16 * LANES), BF), out2=pltpu.VMEM((3 * C, 16 * LANES), F32),
    wide_b=pltpu.VMEM((9 * C, 12 * LANES), BF), out_b=pltpu.VMEM((3 * C, 12 * LANES), F32),
    lhs2=pltpu.VMEM((3 * C, 12 * LANES), BF), lhs1=pltpu.VMEM((3 * C, 10 * LANES), BF),
    want=pltpu.VMEM((16, 12 * LANES), F32), mask_ref=pltpu.VMEM((3, 8, LANES), F32),
    mask2=pltpu.VMEM((8, 12 * LANES), F32), hid2=pltpu.VMEM((C, 12 * LANES), BF),
    slope2=pltpu.VMEM((C, 12 * LANES), F32), back2=pltpu.VMEM((C, 12 * LANES), F32),
    w1_ref=pltpu.VMEM((3 * C, 9 * C), BF), w2_ref=pltpu.VMEM((3 * C, 9 * C), BF),
    wb_ref=pltpu.VMEM((9 * C, 3 * C), BF), head_ref=pltpu.VMEM((16, C), F32),
    raw_logits=pltpu.VMEM((64, LANES), F32), grads_ref=pltpu.VMEM((2, 32, 16, 128), F32),
    pair_out=pltpu.VMEM((32, 16, 128), BF), pair_in=pltpu.VMEM((32, 16, 128), BF),
    send_buf=pltpu.VMEM((32, 16, 128), BF), rs_buf=pltpu.VMEM((32, 16, 128), BF),
    y_buf=pltpu.VMEM((N_Y, 16, 128), BF), done=pltpu.VMEM((2, 32, 16, 128), BF),
    send_sem=pltpu.SemaphoreType.DMA((64,)), recv_sem=pltpu.SemaphoreType.DMA((2, 32)),
    pair_send=pltpu.SemaphoreType.DMA, pair_sem=pltpu.SemaphoreType.DMA,
    rs_send=pltpu.SemaphoreType.DMA((32,)), rs_sem=pltpu.SemaphoreType.DMA((32,)),
    y_send=pltpu.SemaphoreType.DMA((N_Y,)), y_sem=pltpu.SemaphoreType.DMA((N_Y,)),
    ag_send=pltpu.SemaphoreType.DMA((32,)), ag_sem=pltpu.SemaphoreType.DMA((32,)),
    last_send=pltpu.SemaphoreType.DMA((32,)), last_sem=pltpu.SemaphoreType.DMA((32,)),
)


def whole_kernel(scale, ids_ref, features_ref, targets_ref, k1_ref, k2_ref, head_in_ref,
                 logits_ref, first_ref, second_ref, head_out_ref, *scratch):
    s = SimpleNamespace(**dict(zip(SCRATCH, scratch)))
    sent = gather_stage(
        features_ref, targets_ref, s.got, s.own, s.wants, s.send_sem, s.recv_sem,
        lambda: prepare(s, ids_ref, k1_ref, k2_ref, head_in_ref))
    compute(s, scale)
    grad_sum_stage(s, s.grads_ref, first_ref, second_ref, head_out_ref, lambda: finish_logits(s, logits_ref))
    for one in sent:
        one.wait_send()


def on_device(features, device_block, conv_first, conv_second, head_weight, targets):
    n_dp, n_sp = lax.axis_size("dp"), lax.axis_size("space")
    scale = (n_dp * n_sp * 3 * 512) ** (-0.5)
    vmem = pl.BlockSpec(memory_space=pltpu.VMEM)
    kernel = jax.ShapeDtypeStruct((27, C, C), F32)
    logits, first, second, head = pl.pallas_call(
        functools.partial(whole_kernel, scale),
        out_shape=(jax.ShapeDtypeStruct((3, 512), F32), kernel, kernel, jax.ShapeDtypeStruct((3, C), F32)),
        in_specs=[pl.BlockSpec(memory_space=pltpu.SMEM)] + [vmem] * 5,
        out_specs=(vmem,) * 4,
        scratch_shapes=list(SCRATCH.values()),
        compiler_params=pltpu.CompilerParams(
            collective_id=0, has_side_effects=True, vmem_limit_bytes=60 * 1024 * 1024),
    )(device_block, features, targets, conv_first.transpose(1, 0, 2), conv_second.transpose(1, 0, 2), head_weight)
    return (logits[None, None], first.transpose(1, 0, 2), second.transpose(1, 0, 2), head)


def solution(mesh):
    in_specs = (
        P("dp", "space", None, None),
        P("dp", None),
        P(),
        P(),
        P(),
        P("dp", "space", None, None),
    )
    out_specs = (P("dp", "space", None, None), P(), P(), P())
    return jax.shard_map(
        on_device, mesh=mesh, in_specs=in_specs, out_specs=out_specs, check_vma=False
    )
```

time: 89 us -> 77.4 us (0.87)
  Pallas kernels: 81.9 us -> 70.5 us
    pallas_call x3 -> x1, Pallas kernels: 81.9 us -> 70.5 us  [on_device(): pl.pallas_call(functools.partial(whole_kernel, scale), out_shape=(jax.Sha...]
    unnamed x9 -> x11, local copies, waits for them, and re-layouts: 6.05 us -> 6.04 us
where the time goes in v5:
time: 77.4 us; the launch traced here: 77.2 us
  Pallas kernels  70.5 us (91%)
  local copies, waits for them, and re-layouts  6.04 us (8%)
    pallas_call x1, Pallas kernels, on_device(): pl.pallas_call(functools.partial(whole_kernel, scale), out_shape=(jax.Sha...  70.5 us
    unnamed x11, local copies, waits for them, and re-layouts  6.04 us

profile of v5, /device:TPU:1, one launch (start us, length us, event | category | flops | bytes accessed | tf_op | source)
XLA Modules:
  0.0 77.2 jit_solution(13891552357793078679)
XLA Ops:
  0.6 1.3 %copy.10.targets_ref = s32[1,1,3,512]{3,2,1,0:T(4,128)} copy(s32[1,1,3,512]{3,1,2,0:T(1,128)} %param.11) | data formatting | bytes 12288 | tf_op args[5]
  1.9 70.5 %shard_map.93 = (f32[3,512]{1,0:T(4,128)}, f32[27,48,48]{2,1,0:T(8,128)}, f32[27,48,48]{2,1,0:T(8,128)}, f32[3,48]{1,0:T(4,128)}) custom-call(s32[1,32]{1,0:T(1,128)} %ids_ref.1, bf16[1,1,48,512]{3,2,1,0:T(8,128)(2,1)} %features_ref.1, s32[1,1,3,512]{3,2,1,0:T(4,128)} %copy.10.targets_ref, bf16[27,48,48]{2,1,0:T(8,128)(2,1)} %bitcast.7, ...), custom_call_target="tpu_custom_call" | custom-call | tf_op jit(solution)/shard_map/pallas_call | solution.py:450
  72.4 0.0 copy-start.1
  72.4 0.7 copy-done.1
  73.1 0.6 copy.11
  73.7 0.0 copy-start
  73.7 2.0 %copy.15 = f32[48,27,48]{2,0,1:T(8,128)} copy(f32[48,27,48]{2,0,1:T(8,128)} %bitcast.6) | data formatting | bytes 497664
  75.8 0.0 copy-done
  75.8 0.0 copy-start.2
  75.8 0.8 %copy.16 = f32[48,27,48]{2,0,1:T(8,128)} copy(f32[48,27,48]{2,0,1:T(8,128)S(1)} %bitcast.5) | data formatting | bytes 497664
  76.6 0.0 copy-done.2
  76.6 0.6 copy.17
Async XLA Ops:
  72.4 0.7 copy-start.1
  73.7 2.0 %copy-start = (f32[27,48,48]{2,1,0:T(8,128)S(1)}, f32[27,48,48]{2,1,0:T(8,128)}, u32[]{:S(2)}) copy-start(f32[27,48,48]{2,1,0:T(8,128)} %get-tuple-element.10) | copy-start | bytes 746500
  75.8 0.8 %copy-start.2 = (f32[3,48]{1,0:T(4,128)S(1)}, f32[3,48]{1,0:T(4,128)}, u32[]{:S(2)}) copy-start(f32[3,48]{1,0:T(4,128)} %get-tuple-element.23) | copy-start | bytes 1732

commit v6 on v5

--- a/solution.py
+++ b/solution.py
@@ -65,7 +65,8 @@
     for pair in range(4):
         lanes = slice(pair * 128, (pair + 1) * 128)
         own_ref[pair * C:(pair + 1) * C, :] = features_ref[0, 0, :, lanes]
-        wants[pair * 4:pair * 4 + 3, :] = targets_ref[0, 0, :, lanes].astype(F32)
+        for j in range(3):
+            wants[pair * 4 + j:pair * 4 + j + 1, :] = targets_ref[j * 4 + pair:j * 4 + pair + 1, :].astype(F32)
     own_ref[4 * C:4 * C + 16, :] = wants[...].astype(BF)
     got_ref[sp] = own_ref[...]
     pl.semaphore_wait(barrier, len(near_by) + len(others))
@@ -85,7 +86,12 @@
         one.start()
         sent.append(one)
 
+    arrived = set()
+
     def await_block(half, dz, dx):
+        if (half, dz, dx) in arrived:
+            return
+        arrived.add((half, dz, dx))
         slot = at(dz, dx)
         pltpu.make_async_remote_copy(
             src_ref=own_ref.at[rows[half]], dst_ref=got_ref.at[slot, rows[half]], send_sem=send_sem.at[0],
@@ -203,13 +209,15 @@
     def window(plane_24, start):
         return pltpu.roll(plane_24, 384 - start, 1)[:, :LANES]
 
-    @pl.loop(0, 18)
-    def _(at):
+    def window_plane(at, carry):
         rows = pl.ds(pl.multiple_of(at * C, 16), C)
         for c in range(3):
             tall = jnp.concatenate([s.faces[by, rows, c * 128:(c + 1) * 128] for by in range(3)], axis=1)
             for b in range(3):
                 s.wide1[(b * 3 + c) * C:(b * 3 + c + 1) * C, plane(at)] = window(tall, 48 + 16 * b)
+        return carry
+
+    lax.fori_loop(0, 18, window_plane, 0, unroll=3)
 
     for at in range(6):
         tall = window(jnp.concatenate([one[at * 16:(at + 1) * 16] for one in wanted], axis=1), 64)
@@ -245,7 +253,7 @@
             s.wide2[bc * C:(bc + 1) * C, plane(xo)] = pltpu.roll(hid, shift, 1) if shift else hid
         return carry
 
-    lax.fori_loop(0, 16, first_plane, 0, unroll=2)
+    lax.fori_loop(0, 16, first_plane, 0, unroll=4)
 
     s.out2[...] = dot32(s.w2_ref[...], s.wide2[...])
 
@@ -257,7 +265,7 @@
         s.slope2[:, plane(i)] = slope * mask
         return carry
 
-    lax.fori_loop(0, 12, second_plane, 0, unroll=2)
+    lax.fori_loop(0, 12, second_plane, 0, unroll=4)
     logits = dot32(head, s.hid2[...])
     for x in range(8):
         s.raw_logits[x * 8:(x + 1) * 8, :] = logits[0:8, (x + 2) * LANES:(x + 3) * LANES]
@@ -280,7 +288,7 @@
         grad_plane(i + 2, True)
         return carry
 
-    lax.fori_loop(0, 8, own_plane, 0, unroll=2)
+    lax.fori_loop(0, 8, own_plane, 0, unroll=4)
     for i in (0, 1, 10, 11):
         grad_plane(i, False)
 
@@ -288,13 +296,15 @@
         s.lhs2[...], s.wide2[:, 2 * LANES:14 * LANES], NT, preferred_element_type=F32), jnp.zeros((16, C), F32))
     s.out_b[...] = lax.dot_general(s.wb_ref[...], s.wide_b[...], TN, preferred_element_type=F32)
 
-    @pl.loop(4, 12)
-    def _(q):
+    def last_plane(q, carry):
         back = s.out_b[0:C, plane(q)] + s.out_b[C:2 * C, plane(q - 2)] + s.out_b[2 * C:3 * C, plane(q - 4)]
         _act, slope = elu_pair(s.pre1[q])
         grad_pre = (back * slope * own_lane).astype(BF)
         for a in range(3):
             s.lhs1[a * C:(a + 1) * C, plane(q + a - 4)] = grad_pre
+        return carry
+
+    lax.fori_loop(4, 12, last_plane, 0, unroll=4)
 
     pack_grads(s.grads_ref, 0, lax.dot_general(
         s.lhs1[...], s.wide1[:, 4 * LANES:14 * LANES], NT, preferred_element_type=F32), head_grad)
@@ -311,7 +321,9 @@
     parts = dot32(jnp.concatenate([high, middle, low], axis=0), pick)
     own_logits = (parts[0:64] + parts[64:128]) + parts[128:192]
     for x in range(8):
-        logits_ref[:, x * 64:(x + 1) * 64] = own_logits[x * 8:x * 8 + 3]
+        for j in range(3):
+            row = j * 4 + x // 2
+            logits_ref[row:row + 1, x % 2 * 64:x % 2 * 64 + 64] = own_logits[x * 8 + j:x * 8 + j + 1]
 
 
 def grad_sum_stage(s, g_ref, first_ref, second_ref, head_ref, meanwhile):
@@ -342,6 +354,9 @@
     pair_copy.wait_recv()
     send_buf[...] = (g_ref[core] + pair_in[...].astype(F32)).astype(BF)
 
+    far_first = sorted(range(1, n_sp), key=lambda r: abs(n_sp // 2 - r))
+    y_far_first = sorted(range(1, n_y), key=lambda r: abs(n_y // 2 - r))
+
     def rs_copy(r):
         return remote(send_buf.at[along(r)], rs_buf.at[r], rs_send.at[r], rs_sem.at[r], (dp, along(r)))
 
@@ -355,15 +370,15 @@
         slot = lax.rem(sp - r + n_sp, n_sp)
         return remote(done.at[core, slot], done.at[core, slot], last_send.at[r], last_sem.at[r], partner)
 
-    for r in range(1, n_sp):
+    for r in far_first:
         rs_copy(r).start()
     meanwhile()
     total = g_ref[core, sp] + pair_in[sp].astype(F32)
-    for r in range(1, n_sp):
+    for r in reversed(far_first):
         rs_copy(r).wait_recv()
         total = total + rs_buf[r].astype(F32)
     y_buf[0] = total.astype(BF)
-    for r in range(1, n_y):
+    for r in y_far_first:
         y_copy(r).start()
     for r in range(1, n_y):
         y_copy(r).wait_recv()
@@ -371,10 +386,10 @@
     for d in range(n_y):
         total = total + y_buf[lax.rem(y - d + n_y, n_y)].astype(F32)
     done[core, sp] = total.astype(BF)
-    for r in range(1, n_sp):
+    for r in far_first:
         ag_copy(r).start()
     last_copy(0).start()
-    for r in range(1, n_sp):
+    for r in reversed(far_first):
         slot = lax.rem(sp - r + n_sp, n_sp)
         remote(done.at[core, slot], done.at[core, slot], ag_send.at[r], ag_sem.at[r], (dp, along(r))).wait_recv()
         last_copy(r).start()
@@ -385,9 +400,9 @@
     for part, out in enumerate((first_ref, second_ref)):
         for group in range(9):
             a, rows = group // 3, slice(group % 3 * 16, group % 3 * 16 + 16)
-            tail = done[part, 27 + group // 2].astype(F32)
+            tail = done[part, 27 + group // 2]
             out[a * 9 + 8, rows, :] = tail[:, 64 * (group % 2):64 * (group % 2) + C]
-            wide = jnp.concatenate([done[part, group * 3 + col].astype(F32) for col in range(3)], axis=1)
+            wide = jnp.concatenate([done[part, group * 3 + col] for col in range(3)], axis=1)
             for bc in range(8):
                 out[a * 9 + bc, rows, :] = wide[:, bc * C:(bc + 1) * C]
     head_ref[...] = done[0, 31].astype(F32)[0:3, 64:64 + C]
@@ -446,17 +461,18 @@
     n_dp, n_sp = lax.axis_size("dp"), lax.axis_size("space")
     scale = (n_dp * n_sp * 3 * 512) ** (-0.5)
     vmem = pl.BlockSpec(memory_space=pltpu.VMEM)
-    kernel = jax.ShapeDtypeStruct((27, C, C), F32)
+    kernel = jax.ShapeDtypeStruct((27, C, C), BF)
     logits, first, second, head = pl.pallas_call(
         functools.partial(whole_kernel, scale),
-        out_shape=(jax.ShapeDtypeStruct((3, 512), F32), kernel, kernel, jax.ShapeDtypeStruct((3, C), F32)),
+        out_shape=(jax.ShapeDtypeStruct((12, 128), F32), kernel, kernel, jax.ShapeDtypeStruct((3, C), F32)),
         in_specs=[pl.BlockSpec(memory_space=pltpu.SMEM)] + [vmem] * 5,
         out_specs=(vmem,) * 4,
         scratch_shapes=list(SCRATCH.values()),
         compiler_params=pltpu.CompilerParams(
             collective_id=0, has_side_effects=True, vmem_limit_bytes=60 * 1024 * 1024),
-    )(device_block, features, targets, conv_first.transpose(1, 0, 2), conv_second.transpose(1, 0, 2), head_weight)
-    return (logits[None, None], first.transpose(1, 0, 2), second.transpose(1, 0, 2), head)
+    )(device_block, features, targets.reshape(12, 128), conv_first.transpose(1, 0, 2), conv_second.transpose(1, 0, 2), head_weight)
+    return (
+        logits.reshape(1, 1, 3, 512), first.transpose(1, 0, 2).astype(F32), second.transpose(1, 0, 2).astype(F32), head)
 
 
 def solution(mesh):

time: 77.4 us -> 75.6 us (0.977)
  other arithmetic: 0 us -> 2.94 us
  local copies, waits for them, and re-layouts: 6.04 us -> 3.15 us
  Pallas kernels: 70.5 us -> 68.6 us
    unnamed x11 -> x3, local copies, waits for them, and re-layouts: 6.04 us -> 1.24 us
    convert_element_type x0 -> x1, other arithmetic: none -> 2.22 us  [on_device(): second.transpose(1, 0, 2).astype(F32)]
    pallas_call x1, Pallas kernels: 70.5 us -> 68.6 us  [on_device(): pl.pallas_call(functools.partial(whole_kernel, scale), out_shape=(jax.Sha...]
    reshape x0 -> x2, local copies, waits for them, and re-layouts: none -> 1.91 us  [the longest x1 1.3 us: on_device(): logits.reshape(1, 1, 3, 512)]
where the time goes in v6:
time: 75.6 us; the launch traced here: 75.3 us
  Pallas kernels  68.6 us (91%)
  local copies, waits for them, and re-layouts  3.15 us (4%)
  other arithmetic  2.94 us (4%)
    pallas_call x1, Pallas kernels, on_device(): pl.pallas_call(functools.partial(whole_kernel, scale), out_shape=(jax.Sha...  68.6 us
    convert_element_type x1, other arithmetic, on_device(): second.transpose(1, 0, 2).astype(F32)  2.22 us

profile of v6, /device:TPU:1, one launch (start us, length us, event | category | flops | bytes accessed | tf_op | source)
XLA Modules:
  0.0 75.3 jit_solution(3382481233608399642)
XLA Ops:
  0.6 0.7 reduce
  1.4 0.6 reshape.14.targets_ref
  2.0 68.6 %shard_map.93 = (f32[12,128]{1,0:T(8,128)}, bf16[27,48,48]{2,1,0:T(8,128)(2,1)}, bf16[27,48,48]{2,1,0:T(8,128)(2,1)}, f32[3,48]{1,0:T(4,128)}) custom-call(s32[1,32]{1,0:T(1,128)} %ids_ref.1, bf16[1,1,48,512]{3,2,1,0:T(8,128)(2,1)} %features_ref.1, s32[12,128]{1,0:T(8,128)} %reshape.14.targets_ref, bf16[27,48,48]{2,1,0:T(8,128)(2,1)} %bitcast.6, ...), custom_call_target="tpu_custom_call" | custom-call | tf_op jit(solution)/shard_map/pallas_call | solution.py:465
  70.5 1.3 %reshape.16 = f32[1,1,3,512]{3,1,2,0:T(1,128)} reshape(f32[12,128]{1,0:T(8,128)} %get-tuple-element.8) | data formatting | bytes 12288 | tf_op jit(solution)/shard_map/reshape | solution.py:475
  71.8 2.2 %convert_bitcast_fusion = (f32[48,27,48]{2,0,1:T(8,128)}, f32[48,27,48]{2,0,1:T(8,128)}) fusion(bf16[27,48,48]{2,1,0:T(8,128)(2,1)} %get-tuple-element.10, bf16[27,48,48]{2,1,0:T(8,128)(2,1)} %get-tuple-element.9), kind=kLoop, calls=%fused_computation | loop fusion | flops 124416 | bytes 746496 | tf_op jit(solution)/shard_map/convert_element_type | solution.py:475
  74.0 0.0 copy-start
  74.0 0.7 copy-done
  74.7 0.6 copy.13
Async XLA Ops:
  74.0 0.7 copy-start

commit v7 on v6

--- a/solution.py
+++ b/solution.py
@@ -311,6 +311,8 @@
 
 
 def finish_logits(s, logits_ref):
+    logits_ref[12:16, :] = jnp.zeros((4, 128), F32)
+
     high = s.raw_logits[...].astype(BF)
     rest = s.raw_logits[...] - high.astype(F32)
     middle = rest.astype(BF)
@@ -405,7 +407,7 @@
             wide = jnp.concatenate([done[part, group * 3 + col] for col in range(3)], axis=1)
             for bc in range(8):
                 out[a * 9 + bc, rows, :] = wide[:, bc * C:(bc + 1) * C]
-    head_ref[...] = done[0, 31].astype(F32)[0:3, 64:64 + C]
+    head_ref[12:15, 0:C] = done[0, 31].astype(F32)[0:3, 64:64 + C]
 
     pair_copy.wait_send()
     for r in range(1, n_sp):
@@ -446,13 +448,13 @@
 
 
 def whole_kernel(scale, ids_ref, features_ref, targets_ref, k1_ref, k2_ref, head_in_ref,
-                 logits_ref, first_ref, second_ref, head_out_ref, *scratch):
+                 rows_ref, first_ref, second_ref, *scratch):
     s = SimpleNamespace(**dict(zip(SCRATCH, scratch)))
     sent = gather_stage(
         features_ref, targets_ref, s.got, s.own, s.wants, s.send_sem, s.recv_sem,
         lambda: prepare(s, ids_ref, k1_ref, k2_ref, head_in_ref))
     compute(s, scale)
-    grad_sum_stage(s, s.grads_ref, first_ref, second_ref, head_out_ref, lambda: finish_logits(s, logits_ref))
+    grad_sum_stage(s, s.grads_ref, first_ref, second_ref, rows_ref, lambda: finish_logits(s, rows_ref))
     for one in sent:
         one.wait_send()
 
@@ -462,17 +464,18 @@
     scale = (n_dp * n_sp * 3 * 512) ** (-0.5)
     vmem = pl.BlockSpec(memory_space=pltpu.VMEM)
     kernel = jax.ShapeDtypeStruct((27, C, C), BF)
-    logits, first, second, head = pl.pallas_call(
+    rows, first, second = pl.pallas_call(
         functools.partial(whole_kernel, scale),
-        out_shape=(jax.ShapeDtypeStruct((12, 128), F32), kernel, kernel, jax.ShapeDtypeStruct((3, C), F32)),
+        out_shape=(jax.ShapeDtypeStruct((16, 128), F32), kernel, kernel),
         in_specs=[pl.BlockSpec(memory_space=pltpu.SMEM)] + [vmem] * 5,
-        out_specs=(vmem,) * 4,
+        out_specs=(vmem,) * 3,
         scratch_shapes=list(SCRATCH.values()),
         compiler_params=pltpu.CompilerParams(
             collective_id=0, has_side_effects=True, vmem_limit_bytes=60 * 1024 * 1024),
     )(device_block, features, targets.reshape(12, 128), conv_first.transpose(1, 0, 2), conv_second.transpose(1, 0, 2), head_weight)
     return (
-        logits.reshape(1, 1, 3, 512), first.transpose(1, 0, 2).astype(F32), second.transpose(1, 0, 2).astype(F32), head)
+        rows[:12].reshape(1, 1, 3, 512), first.transpose(1, 0, 2).astype(F32), second.transpose(1, 0, 2).astype(F32),
+        rows[12:15, :C])
 
 
 def solution(mesh):

time: 75.6 us -> 74.9 us (level)
    slice x0 -> x1, local copies, waits for them, and re-layouts: none -> 1.33 us  [on_device(): rows[12:15, :C]]
    unnamed x3 -> x2, local copies, waits for them, and re-layouts: 1.24 us -> 0.01 us
where the time goes in v7:
time: 74.9 us; the launch traced here: 74.7 us
  Pallas kernels  68.6 us (92%)
  other arithmetic  2.94 us (4%)
  local copies, waits for them, and re-layouts  2.54 us (3%)
    pallas_call x1, Pallas kernels, on_device(): pl.pallas_call(functools.partial(whole_kernel, scale), out_shape=(jax.Sha...  68.6 us
    convert_element_type x1, other arithmetic, on_device(): second.transpose(1, 0, 2).astype(F32)  2.22 us

profile of v7, /device:TPU:1, one launch (start us, length us, event | category | flops | bytes accessed | tf_op | source)
XLA Modules:
  0.0 74.7 jit_solution(10893078404971332028)
XLA Ops:
  0.6 0.7 reduce
  1.4 0.6 reshape.14.targets_ref
  2.0 68.6 %shard_map.93 = (f32[16,128]{1,0:T(8,128)}, bf16[27,48,48]{2,1,0:T(8,128)(2,1)}, bf16[27,48,48]{2,1,0:T(8,128)(2,1)}) custom-call(s32[1,32]{1,0:T(1,128)} %ids_ref.1, bf16[1,1,48,512]{3,2,1,0:T(8,128)(2,1)} %features_ref.1, s32[12,128]{1,0:T(8,128)} %reshape.14.targets_ref, bf16[27,48,48]{2,1,0:T(8,128)(2,1)} %bitcast.7, bf16[27,48,48]{2,1,0:T(8,128)(2,1)} %bitcast.8, ...), custom_call_target="tpu_custom_call" | custom-call | tf_op jit(solution)/shard_map/pallas_call | solution.py:467
  70.5 0.0 copy-start
  70.5 1.3 %slice.7 = f32[3,48]{1,0:T(4,128)} slice(f32[16,128]{1,0:T(8,128)} %get-tuple-element.7), slice={[12:15], [0:48]} | slice | bytes 1152 | tf_op jit(solution)/shard_map/slice | solution.py:478
  71.9 0.0 copy-done
  71.9 0.6 reshape.16
  72.5 2.2 %convert_bitcast_fusion = (f32[48,27,48]{2,0,1:T(8,128)}, f32[48,27,48]{2,0,1:T(8,128)}) fusion(bf16[27,48,48]{2,1,0:T(8,128)(2,1)} %get-tuple-element.9, bf16[27,48,48]{2,1,0:T(8,128)(2,1)} %get-tuple-element.8), kind=kLoop, calls=%fused_computation | loop fusion | flops 124416 | bytes 746496 | tf_op jit(solution)/shard_map/convert_element_type | solution.py:477
Async XLA Ops:
  70.5 1.3 %copy-start = (f32[16,128]{1,0:T(8,128)S(1)}, f32[16,128]{1,0:T(8,128)}, u32[]{:S(2)}) copy-start(f32[16,128]{1,0:T(8,128)} %get-tuple-element.7) | copy-start | bytes 24580
